TPU v7x, 32 devices: a whole 2x2x4 slice. The times are simulated.
32 devices in a mesh: struct: 4 (over y, x), fluid: 8 (over z, core).
Axes of the slice: x: 2, y: 2, z: 4, core: 2. Of those that a mesh axis runs over, the one named last changes fastest.
Arguments:
- shell_motion: float32 [3, 262144], P(None, ('struct', 'fluid')), may hold values from -6 to 6
- owner: int32 [262144, 1], P(('struct', 'fluid')), may hold values from 0 to 31; in each aligned block of 8192 rows (0 to 8191, 8192 to 16383, ...) at most 512 rows name the same one
- stencil_slot: int32 [4, 8, 64, 128], P(None, 'struct', 'fluid'), may hold values from 0 to 16383
- stencil_weight: float32 [4, 8, 64, 128], P(None, 'struct', 'fluid'), may hold values from 0 to 0.5
- prev_motion: float32 [3, 8, 64, 256], P(None, 'struct', 'fluid'), may hold values from -6 to 6
- node_offset: float32 [3, 8, 64, 256], P(None, 'struct', 'fluid'), may hold values from -0.07 to 0.07
- cell_split: int32 [8, 64, 256], P('struct', 'fluid'), may hold values from 0 to 3
Outputs:
- mesh_motion: float32 [3, 8, 64, 256], P(None, 'struct', 'fluid')
Inputs may be any that keep to these rules, and one draw needn't show every extreme that they name: Among the 8192 shell nodes of one device, no owner is named by more than 512 of them, a bound that some block reaches.
All inputs are finite; a program needn't handle non-finite values.
Results may differ from a plain program's by a relative error of at most 0.0003.
Values sent between devices are 32-bit elements; how exact they have to be, the bound alone decides.
A program may use at most 64 MiB of HBM per device.

v0:
```python
import functools

import jax
import jax.numpy as jnp
from jax import lax
from jax.experimental import pallas as pl
from jax.experimental.pallas import tpu as pltpu
from jax.sharding import PartitionSpec as P

SWEEPS = 4
LANES = 128
LAMBDA_RATIO = 1.0
RELAX_FACTOR = 0.5
STEP_ORDERS = ((0, 1, 2), (0, 2, 1), (1, 0, 2), (1, 2, 0), (2, 0, 1), (2, 1, 0))
CORNERS = tuple((a, b, c) for a in (0, 1) for b in (0, 1) for c in (0, 1))
COLUMNS = 16
MESH = pl.DeviceIdType.MESH
BF16 = jnp.bfloat16
F32 = jnp.float32


def split_two(values):
    high = values.astype(BF16)
    low = (values - high.astype(F32)).astype(BF16)
    return high, low


def iota(shape, dim):
    return lax.broadcasted_iota(jnp.int32, shape, dim)


def swap_corners(corners, flip_y, flip_z):
    middle = {}
    for a, b, c in CORNERS:
        middle[a, b, c] = [
            jnp.where(flip_y, q, p) for p, q in zip(corners[a, b, c], corners[a, 1 - b, c])
        ]
    return {
        (a, b, c): [jnp.where(flip_z, q, p) for p, q in zip(middle[a, b, c], middle[a, b, 1 - c])]
        for a, b, c in CORNERS
    }


def paths():
    for order in STEP_ORDERS:
        position, path = [0, 0, 0], []
        for axis_id in order:
            position[axis_id] = 1
            path.append(tuple(position))
        yield path


def cross(p, q):
    return [p[1] * q[2] - p[2] * q[1], p[2] * q[0] - p[0] * q[2], p[0] * q[1] - p[1] * q[0]]


def add_to(table, key, vector):
    table[key] = [p + q for p, q in zip(table[key], vector)] if key in table else list(vector)


def cell_gradients(offsets, flip_y, flip_z):
    offsets = swap_corners(offsets, flip_y, flip_z)
    sign_y, sign_z = jnp.where(flip_y, -1.0, 1.0), jnp.where(flip_z, -1.0, 1.0)
    anchor = offsets[0, 0, 0]
    edges = {}
    for vertex in CORNERS[1:]:
        edge = [p - q for p, q in zip(offsets[vertex], anchor)]
        if vertex[0]:
            edge[0] = edge[0] + 1.0
        if vertex[1]:
            edge[1] = edge[1] + sign_y
        if vertex[2]:
            edge[2] = edge[2] + sign_z
        edges[vertex] = edge
    gradients, diagonal = [], {}
    for path in paths():
        one, two, three = [edges[v] for v in path]
        across = [cross(two, three), cross(three, one), cross(one, two)]
        volume = one[0] * across[0][0] + one[1] * across[0][1] + one[2] * across[0][2]
        inverse = 1.0 / volume
        grads = [[p * inverse for p in vector] for vector in across]
        gradients.append(grads)
        first = [-(grads[0][p] + grads[1][p] + grads[2][p]) for p in range(3)]
        for vertex, grad in zip([(0, 0, 0)] + path, [first] + grads):
            square = [p * p for p in grad]
            norm = square[0] + square[1] + square[2]
            add_to(diagonal, vertex, [(LAMBDA_RATIO + 1.0) * p + norm for p in square])
    return gradients, swap_corners(diagonal, flip_y, flip_z)


def cell_forces(gradients, motion, flip_y, flip_z):
    motion = swap_corners(motion, flip_y, flip_z)
    anchor = motion[0, 0, 0]
    moves = {v: [p - q for p, q in zip(motion[v], anchor)] for v in CORNERS[1:]}
    forces = {}
    for tet, path in enumerate(paths()):
        grads = [[gradients(tet, v, p) for p in range(3)] for v in range(3)]
        tensor = [
            [
                moves[path[0]][p] * grads[0][q]
                + moves[path[1]][p] * grads[1][q]
                + moves[path[2]][p] * grads[2][q]
                for q in range(3)
            ]
            for p in range(3)
        ]
        trace = LAMBDA_RATIO * (tensor[0][0] + tensor[1][1] + tensor[2][2])
        stress = [[None] * 3 for _ in range(3)]
        for p in range(3):
            stress[p][p] = tensor[p][p] + tensor[p][p] + trace
            for q in range(p):
                stress[p][q] = stress[q][p] = tensor[p][q] + tensor[q][p]
        for v in range(3):
            add_to(
                forces,
                path[v],
                [
                    stress[p][0] * grads[v][0] + stress[p][1] * grads[v][1] + stress[p][2] * grads[v][2]
                    for p in range(3)
                ],
            )
    first = None
    for vector in forces.values():
        first = vector if first is None else [p + q for p, q in zip(first, vector)]
    forces[0, 0, 0] = [-p for p in first]
    return swap_corners(forces, flip_y, flip_z)


def turn(x, shift, axis):
    shift %= x.shape[axis]
    return pltpu.roll(x, shift, axis) if shift else x


def float_codes(value):
    return value >= 1.5, (value == 1.0) | (value == 3.0)


def int_codes(value):
    return value >= 2, (value & 1) == 1


def corners_of(low, high):
    corners = {}
    for b, row in ((0, low), (1, high)):
        for a in (0, 1):
            far = [turn(p, -a, 1) for p in row]
            corners[a, b, 0] = far
            corners[a, b, 1] = [turn(p, -1, 0) for p in far]
    return corners


def assemble_row(parts, b):
    near = [p + turn(q, 1, 0) for p, q in zip(parts[0, b, 0], parts[0, b, 1])]
    far = [p + turn(q, 1, 0) for p, q in zip(parts[1, b, 0], parts[1, b, 1])]
    return [p + turn(q, 1, 1) for p, q in zip(near, far)]


def merge_planes(left, own, right, depth):
    return jnp.concatenate([left[left.shape[0] - depth :], own, right[:depth]], axis=0)


def place_nodes(devices, capacity, own_ref, place_ref):
    rows = own_ref.shape[0]
    own = own_ref[...]
    upper = (iota((LANES, LANES), 0) < iota((LANES, LANES), 1)).astype(F32)
    prefix_all = jnp.concatenate([upper, jnp.ones((LANES, LANES), F32)], axis=1).astype(BF16)
    lower = (iota((rows, rows), 1) < iota((rows, rows), 0)).astype(F32).astype(BF16)
    chunk = min(devices, 32)

    def ranks(step, place):
        for o in range(chunk):
            target = step * chunk + o
            named = own == target
            both = jnp.dot(named.astype(F32).astype(BF16), prefix_all, preferred_element_type=F32)
            ahead = jnp.dot(lower, both[:, LANES:].astype(BF16), preferred_element_type=F32)
            rank = (both[:, :LANES] + ahead).astype(jnp.int32)
            place = jnp.where(named, rank + target * capacity, place)
        return place

    place = jnp.zeros((rows, LANES), jnp.int32)
    if chunk == devices:
        place = ranks(0, place)
    else:
        place = lax.fori_loop(0, devices // chunk, ranks, place)
    place_ref[...] = place


def pack_nodes(first, last, place_ref, val_ref, acc_ref):
    wide = 2 * LANES
    groups = acc_ref.shape[0] // 3
    group_id = iota((groups, LANES), 0)
    lane_id = iota((wide, LANES), 0)

    def spread(step, carry):
        total = None
        for u in range(4):
            row = step * 4 + u
            at = place_ref[pl.ds(row, 1), :]
            hit = group_id == at // wide
            column = (lane_id == at % wide).astype(F32).astype(BF16)
            parts = []
            for c in range(3):
                value = val_ref[pl.ds(c, 1), pl.ds(pl.multiple_of(row * LANES, LANES), LANES)]
                high = value.astype(BF16).astype(F32)
                low = value - high
                parts.append(
                    jnp.concatenate(
                        [jnp.where(hit, high, 0.0).astype(BF16), jnp.where(hit, low, 0.0).astype(BF16)],
                        axis=1,
                    )
                )
            left = jnp.concatenate(parts, axis=0)
            right = jnp.concatenate([column, column], axis=1)
            product = lax.dot_general(
                left, right, (((1,), (1,)), ((), ())), preferred_element_type=F32
            )
            total = product if total is None else total + product
        acc_ref[...] += total
        return carry

    lax.fori_loop(first, last, spread, 0)


def window_kernel(
    counts,
    shell,
    owner,
    slot,
    weight,
    prev,
    offset,
    split,
    out,
    v_shell,
    v_owner,
    v_slot,
    v_weight,
    near_offset,
    near_split,
    near_motion,
    wall_offset,
    wall_split,
    place,
    acc,
    packed,
    received,
    table,
    both,
    v_wall,
    edge_in,
    wall_in,
    edge_field,
    edge_grad,
    edge_diag,
    edge_motion,
    motion,
    force,
    node_offset,
    cell_code,
    grad,
    diag,
    local_sem,
    near_send,
    near_recv,
    edge_send,
    edge_recv,
    row_send,
    row_recv,
    pack_send,
    pack_recv,
    wall_send,
    wall_recv,
):
    num_struct, num_fluid = counts
    devices = num_struct * num_fluid
    s, f = lax.axis_index("struct"), lax.axis_index("fluid")
    me = s * num_fluid + f
    stencil, count_y, count_z, wall = slot.shape
    free = prev.shape[3] - wall
    nodes = count_y * count_z
    deep = count_z + 2 * SWEEPS
    span = count_y * COLUMNS
    rows_own = v_owner.shape[0]
    capacity = 2 * rows_own * LANES // devices
    pieces = capacity // LANES
    groups = devices * pieces
    half = LANES // 2
    last_y = count_y - 1

    def peer(ds, df):
        return ((s + ds + num_struct) % num_struct, (f + df + num_fluid) % num_fluid)

    def remote(src, dst, send, recv, where):
        return pltpu.make_async_remote_copy(
            src_ref=src, dst_ref=dst, send_sem=send, recv_sem=recv, device_id=where, device_id_type=MESH
        )

    free_lanes, wall_lanes = pl.ds(wall, free), pl.ds(0, wall)
    loads = [
        (owner, v_owner),
        (offset.at[:, :, :, free_lanes], near_offset.at[4]),
        (split.at[:, :, free_lanes], near_split.at[4]),
        (prev.at[:, :, :, free_lanes], near_motion.at[4]),
        (offset.at[:, :, :, wall_lanes], wall_offset),
        (split.at[:, :, wall_lanes], wall_split),
        (shell, v_shell),
        (slot, v_slot),
        (weight, v_weight),
    ]
    loads = [pltpu.make_async_copy(a, b, local_sem.at[n]) for n, (a, b) in enumerate(loads)]
    for load in loads:
        load.start()

    barrier = pltpu.get_barrier_semaphore()

    def greet(d, carry):
        other = (me + d) % devices
        pl.semaphore_signal(
            barrier, inc=1, device_id=(other // num_fluid, other % num_fluid), device_id_type=MESH
        )
        return carry

    lax.fori_loop(1, devices, greet, 0)

    loads[0].wait()
    place_nodes(devices, capacity, v_owner, place)
    for load in loads[1:6]:
        load.wait()

    lane8 = iota((count_z, LANES), 1)
    own_tiles = [jnp.zeros((count_z, LANES), F32) for _ in range(4)]
    for n in range(7):
        for j in range(count_y):
            if n < 3:
                a, w = near_offset[4, n, j], wall_offset[n, j]
            elif n == 3:
                a, w = near_split[4, j].astype(F32), wall_split[j].astype(F32)
            else:
                a = near_motion[4, n - 4, j]
                w = a
            for side in (0, 1):
                base = half * (n % 2) + span * side + COLUMNS * j
                if side == 0:
                    joined = turn(jnp.where(lane8 == LANES - 1, w, a), base + 1, 1)
                else:
                    joined = turn(jnp.where(lane8 == 0, w, a), base + 2 * SWEEPS, 1)
                inside = (lane8 >= base) & (lane8 < base + COLUMNS)
                own_tiles[n // 2] = jnp.where(inside, joined, own_tiles[n // 2])
    for n in range(4):
        edge_in[0, 1, n] = own_tiles[n]

    pl.semaphore_wait(barrier, devices - 1)

    def near_copies(ds, df, at):
        src, dst = 4, (1 - ds) * 3 + 1 - df
        if at is not None:
            dst = at
        lines = pl.ds(0, count_y) if ds == 0 else pl.ds(last_y if ds > 0 else 0, 1)
        if at is not None and ds != 0:
            lines = pl.ds(last_y if ds < 0 else 0, 1)
        send = (ds + 1) * 3 + df + 1
        return [
            remote(
                near_offset.at[src, :, lines],
                near_offset.at[dst, :, lines],
                near_send.at[send, 0],
                near_recv.at[dst, 0],
                peer(ds, df),
            ),
            remote(
                near_split.at[src, lines],
                near_split.at[dst, lines],
                near_send.at[send, 1],
                near_recv.at[dst, 1],
                peer(ds, df),
            ),
            remote(
                near_motion.at[src, :, lines],
                near_motion.at[dst, :, lines],
                near_send.at[send, 2],
                near_recv.at[dst, 2],
                peer(ds, df),
            ),
        ]

    around = [(ds, df) for ds in (-1, 0, 1) for df in (-1, 0, 1) if (ds, df) != (0, 0)]
    near_out = [copy for ds, df in around for copy in near_copies(ds, df, None)]
    near_back = [copy for ds, df in around for copy in near_copies(ds, df, (ds + 1) * 3 + df + 1)]
    for copy in near_out:
        copy.start()

    wide_around = [(r, df) for r in range(num_struct) for df in (-1, 0, 1) if (r, df) != (0, 0)]

    def wide_copies(buffer, send, recv):
        return [
            remote(
                buffer.at[0, 1],
                buffer.at[r, df + 1],
                send.at[r * 3 + df + 1],
                recv.at[r * 3 + df + 1],
                peer(-r, -df),
            )
            for r, df in wide_around
        ]

    edge_copies = wide_copies(edge_in, edge_send, edge_recv)
    for copy in edge_copies:
        copy.start()

    def row_copies(sweep):
        return [
            remote(motion.at[sweep, 1], motion.at[sweep, 3], row_send.at[sweep, 0], row_recv.at[sweep, 0], peer(-1, 0)),
            remote(motion.at[sweep, 2], motion.at[sweep, 0], row_send.at[sweep, 1], row_recv.at[sweep, 1], peer(1, 0)),
        ]

    def prepare_main():
        for r in range(count_y + 2):
            ds, j = (-1, last_y) if r == 0 else (1, 0) if r == count_y + 1 else (0, r - 1)
            at = [(ds + 1) * 3 + df + 1 for df in (-1, 0, 1)]
            for c in range(3):
                node_offset[r, c] = merge_planes(*[near_offset[n, c, j] for n in at], SWEEPS)
                motion[0, r, c] = merge_planes(*[near_motion[n, c, j] for n in at], SWEEPS)
            cell_code[r] = merge_planes(*[near_split[n, j] for n in at], SWEEPS)
        diag[...] = jnp.zeros_like(diag)

        def row(j, carry):
            flip_y, flip_z = int_codes(cell_code[j])
            corners = corners_of(
                [node_offset[j, c] for c in range(3)], [node_offset[j + 1, c] for c in range(3)]
            )
            gradients, parts = cell_gradients(corners, flip_y, flip_z)
            for tet in range(6):
                for v in range(3):
                    for p in range(3):
                        grad[j, 9 * tet + 3 * v + p] = gradients[tet][v][p]
            for b in (0, 1):
                for c, value in enumerate(assemble_row(parts, b)):
                    diag[j + b, c] = diag[j + b, c] + value
            return carry

        lax.fori_loop(0, count_y + 1, row, 0)

    def sweep_main(sweep):
        force[...] = jnp.zeros_like(force)

        def row(j, carry):
            flip_y, flip_z = int_codes(cell_code[j])
            corners = corners_of(
                [motion[sweep, j, c] for c in range(3)], [motion[sweep, j + 1, c] for c in range(3)]
            )
            parts = cell_forces(lambda tet, v, p: grad[j, 9 * tet + 3 * v + p], corners, flip_y, flip_z)
            for b in (0, 1):
                for c, value in enumerate(assemble_row(parts, b)):
                    force[j + b, c] = force[j + b, c] + value
            return carry

        lax.fori_loop(0, count_y + 1, row, 0)
        for r in range(1, count_y + 1):
            for c in range(3):
                motion[sweep + 1, r, c] = motion[sweep, r, c] - RELAX_FACTOR * force[r, c] / diag[r, c]

    lane_deep = iota((deep, LANES), 1)
    lane_edge = iota((2 * deep, LANES), 1)

    def wide_merge(read):
        return [merge_planes(read(r, 0), read(r, 1), read(r, 2), SWEEPS) for r in range(num_struct)]

    def edge_corners(values):
        corners = {}
        for a in (0, 1):
            for b in (0, 1):
                shifted = [turn(p, -a - COLUMNS * b, 1) for p in values]
                corners[a, b, 0] = shifted
                corners[a, b, 1] = [turn(p, -1, 0) for p in shifted]
        return corners

    def edge_assemble(parts):
        low, high = assemble_row(parts, 0), assemble_row(parts, 1)
        return [p + turn(q, COLUMNS, 1) for p, q in zip(low, high)]

    def prepare_edge():
        for tile in range(4):
            merged = wide_merge(lambda r, d: edge_in[r, d, tile])
            for n in (2 * tile, 2 * tile + 1):
                if n == 7:
                    continue
                for side in (0, 1):
                    base = half * (n % 2) + span * side
                    total = None
                    for r in range(num_struct):
                        moved = turn(merged[r], span * r - base, 1)
                        total = moved if total is None else jnp.where(lane_deep >= span * r, moved, total)
                    edge_field[n, pl.ds(deep * side, deep), :] = total
        flip_y, flip_z = float_codes(edge_field[3])
        gradients, parts = cell_gradients(edge_corners([edge_field[c] for c in range(3)]), flip_y, flip_z)
        for tet in range(6):
            for v in range(3):
                for p in range(3):
                    edge_grad[9 * tet + 3 * v + p] = gradients[tet][v][p]
        for c, value in enumerate(edge_assemble(parts)):
            edge_diag[c] = value

    def plane_points(ref, zero):
        row, lane = iota((nodes, LANES), 0), iota((nodes, LANES), 1)
        within = row // count_z * (2 * count_z) + count_z - 1 - row % count_z
        total = None
        for t in range(stencil):
            whole = jnp.concatenate([ref[t, j] for j in range(count_y)], axis=0)
            for side in (0, 1):
                column = wall - 1 if side == 0 else 0
                spread = jnp.broadcast_to(whole[:, column : column + 1], (nodes, LANES))
                part = jnp.where(lane == 2 * nodes * t + count_z * side + within, spread, zero)
                total = part if total is None else total + part
        return jnp.sum(total, axis=0, keepdims=True)

    acc[...] = jnp.zeros_like(acc)
    loads[6].wait()
    steps = rows_own // 4
    pack_nodes(0, steps // 2, place, v_shell, acc)
    for copy in near_back:
        copy.wait_recv()
    prepare_main()
    sweep_main(0)
    for copy in row_copies(1):
        copy.start()
    pack_nodes(steps // 2, steps, place, v_shell, acc)
    pack_groups = groups // 2
    for o in range(devices):
        for c in range(3):
            for b in range(pieces):
                m = o * pieces + b
                packed[o, pl.ds(c * pieces + b, 1), :] = acc[
                    pl.ds(c * pack_groups + m // 2, 1), pl.ds((m % 2) * LANES, LANES)
                ]

    def pack_copy(other):
        return remote(
            packed.at[other],
            received.at[me],
            pack_send.at[other],
            pack_recv.at[me],
            (other // num_fluid, other % num_fluid),
        )

    def pack_arrival(other):
        return remote(
            packed.at[other],
            received.at[other],
            pack_send.at[other],
            pack_recv.at[other],
            (other // num_fluid, other % num_fluid),
        )

    def send_pack(d, carry):
        pack_copy((me + d) % devices).start()
        return carry

    lax.fori_loop(1, devices, send_pack, 0)
    received[me] = packed[me]

    for copy in edge_copies:
        copy.wait_recv()
    prepare_edge()
    for copy in row_copies(1):
        copy.wait_recv()
    sweep_main(1)
    for copy in row_copies(2):
        copy.start()
    loads[7].wait()
    loads[8].wait()
    plane_slot, plane_weight = plane_points(v_slot, 0), plane_points(v_weight, 0.0)
    for copy in row_copies(2):
        copy.wait_recv()
    sweep_main(2)
    for copy in row_copies(3):
        copy.start()

    def await_pack(d, carry):
        pack_arrival((me + d) % devices).wait_recv()
        return carry

    lax.fori_loop(1, devices, await_pack, 0)

    for c in range(3):
        for o in range(devices):
            table[pl.ds(c * groups + o * pieces, pieces), :] = received[o, pl.ds(c * pieces, pieces), :]
    high, low = split_two(table[...])
    both[:, :LANES] = high
    both[:, LANES:] = low

    pick = (iota((LANES, LANES), 0) == plane_slot % LANES).astype(F32).astype(BF16)
    found = jnp.dot(both[...], jnp.concatenate([pick, pick], axis=0), preferred_element_type=F32)
    scaled = jnp.where(iota((groups, LANES), 0) == plane_slot // LANES, plane_weight, 0.0)
    tile = jnp.zeros((count_z, LANES), F32)
    for c in range(3):
        line = jnp.sum(found[c * groups : (c + 1) * groups] * scaled, axis=0, keepdims=True)
        period = LANES // 2
        while period >= 2 * nodes:
            line = line + turn(line, period, 1)
            period //= 2
        spread = pltpu.roll(jnp.broadcast_to(line, (count_z, LANES)), 0, 1, stride=1, stride_axis=0)
        tile = jnp.where((lane8 >= span * c) & (lane8 < span * (c + 1)), spread, tile)
    wall_in[0, 1] = tile
    wall_copies = wide_copies(wall_in, wall_send, wall_recv)
    for copy in wall_copies:
        copy.start()

    wide = 2 * LANES
    lane_id = iota((LANES, wide), 0)
    group_id = iota((groups, wide), 0)

    def pair(step, carry):
        j, k = 2 * step // count_z, 2 * step % count_z
        sums = [None] * 3
        for t in range(stencil):
            at = jnp.concatenate(
                [v_slot[t, j, pl.ds(k, 1), :], v_slot[t, j, pl.ds(k + 1, 1), :]], axis=1
            )
            by = jnp.concatenate(
                [v_weight[t, j, pl.ds(k, 1), :], v_weight[t, j, pl.ds(k + 1, 1), :]], axis=1
            )
            choose = (lane_id == at % LANES).astype(F32).astype(BF16)
            values = jnp.dot(
                both[...], jnp.concatenate([choose, choose], axis=0), preferred_element_type=F32
            )
            factor = jnp.where(group_id == at // LANES, by, 0.0)
            for c in range(3):
                term = values[c * groups : (c + 1) * groups] * factor
                sums[c] = term if sums[c] is None else sums[c] + term
        for c in range(3):
            line = jnp.sum(sums[c], axis=0, keepdims=True)
            v_wall[c, pl.ds(2 * step, 1), :] = line[:, :LANES]
            v_wall[c, pl.ds(2 * step + 1, 1), :] = line[:, LANES:]
        return carry

    lax.fori_loop(0, nodes // 2, pair, 0)

    for copy in row_copies(3):
        copy.wait_recv()
    sweep_main(3)

    for copy in wall_copies:
        copy.wait_recv()
    column = lane_edge % COLUMNS
    second = iota((2 * deep, LANES), 0) >= deep
    wall_column = column == jnp.where(second, 2 * SWEEPS, 0)
    inner = (column >= 1) & (column < 2 * SWEEPS)
    arrived = wide_merge(lambda r, d: wall_in[r, d])
    for c in range(3):
        total = None
        for r in range(num_struct):
            moved = turn(arrived[r], span * (r - c) - (count_z - 1), 1)
            total = moved if total is None else jnp.where(lane_deep >= span * r, moved, total)
        total = jnp.concatenate([total, total], axis=0)
        edge_motion[c] = jnp.where(wall_column, total, edge_field[4 + c])

    def sweep_edge(step, carry):
        flip_y, flip_z = float_codes(edge_field[3])
        parts = cell_forces(
            lambda tet, v, p: edge_grad[9 * tet + 3 * v + p],
            edge_corners([edge_motion[c] for c in range(3)]),
            flip_y,
            flip_z,
        )
        for c, value in enumerate(edge_assemble(parts)):
            now = edge_motion[c]
            edge_motion[c] = jnp.where(inner, now - RELAX_FACTOR * value / edge_diag[c], now)
        return carry

    lax.fori_loop(0, SWEEPS, sweep_edge, 0)

    for c in range(3):
        for j in range(count_y):
            out[c, j, :, wall_lanes] = v_wall[c, pl.ds(j * count_z, count_z), :]
            main = motion[SWEEPS, j + 1, c, SWEEPS : SWEEPS + count_z, :]
            low = turn(edge_motion[c, SWEEPS : SWEEPS + count_z, :], -1 - COLUMNS * j, 1)
            high = turn(
                edge_motion[c, deep + SWEEPS : deep + SWEEPS + count_z, :],
                free - 2 * SWEEPS - COLUMNS * j,
                1,
            )
            main = jnp.where(lane8 < SWEEPS, low, jnp.where(lane8 >= free - SWEEPS, high, main))
            out[c, j, :, free_lanes] = main

    for copy in near_out + edge_copies + wall_copies:
        copy.wait_send()
    for sweep in range(1, SWEEPS):
        for copy in row_copies(sweep):
            copy.wait_send()

    def drain(d, carry):
        pack_copy((me + d) % devices).wait_send()
        return carry

    lax.fori_loop(1, devices, drain, 0)


def shards(shell_motion, owner, stencil_slot, stencil_weight, prev_motion, node_offset, cell_split):
    num_struct, num_fluid = lax.axis_size("struct"), lax.axis_size("fluid")
    devices = num_struct * num_fluid
    own = shell_motion.shape[1]
    pieces = 2 * own // devices // LANES
    groups = devices * pieces
    stencil, count_y, count_z, wall = stencil_slot.shape
    free = prev_motion.shape[3] - wall
    nodes, deep = count_y * count_z, count_z + 2 * SWEEPS
    rows = count_y + 2
    assert wall == free == LANES and count_z == 8 and num_struct >= 3 and num_fluid >= 3
    assert num_struct * count_y * COLUMNS == LANES and 2 * stencil * nodes == LANES and count_y == 2
    vmem, dma = pltpu.VMEM, pltpu.SemaphoreType.DMA
    scratch = [
        vmem((3, own), F32),
        vmem((own // LANES, LANES), jnp.int32),
        vmem((stencil, count_y, count_z, wall), jnp.int32),
        vmem((stencil, count_y, count_z, wall), F32),
        vmem((9, 3, count_y, count_z, free), F32),
        vmem((9, count_y, count_z, free), jnp.int32),
        vmem((9, 3, count_y, count_z, free), F32),
        vmem((3, count_y, count_z, wall), F32),
        vmem((count_y, count_z, wall), jnp.int32),
        vmem((own // LANES, LANES), jnp.int32),
        vmem((3 * groups // 2, 2 * LANES), F32),
        vmem((devices, 3 * pieces, LANES), F32),
        vmem((devices, 3 * pieces, LANES), F32),
        vmem((3 * groups, LANES), F32),
        vmem((3 * groups, 2 * LANES), BF16),
        vmem((3, nodes, wall), F32),
        vmem((num_struct, 3, 4, count_z, LANES), F32),
        vmem((num_struct, 3, count_z, LANES), F32),
        vmem((7, 2 * deep, LANES), F32),
        vmem((54, 2 * deep, LANES), F32),
        vmem((3, 2 * deep, LANES), F32),
        vmem((3, 2 * deep, LANES), F32),
        vmem((SWEEPS + 1, rows, 3, deep, free), F32),
        vmem((rows, 3, deep, free), F32),
        vmem((rows, 3, deep, free), F32),
        vmem((rows, deep, free), jnp.int32),
        vmem((rows - 1, 54, deep, free), F32),
        vmem((rows, 3, deep, free), F32),
        dma((9,)),
        dma((9, 3)),
        dma((9, 3)),
        dma((3 * num_struct,)),
        dma((3 * num_struct,)),
        dma((SWEEPS, 2)),
        dma((SWEEPS, 2)),
        dma((devices,)),
        dma((devices,)),
        dma((3 * num_struct,)),
        dma((3 * num_struct,)),
    ]
    return pl.pallas_call(
        functools.partial(window_kernel, (num_struct, num_fluid)),
        out_shape=jax.ShapeDtypeStruct(prev_motion.shape, F32),
        in_specs=[pl.BlockSpec(memory_space=pltpu.HBM)] * 7,
        out_specs=pl.BlockSpec(memory_space=pltpu.VMEM),
        scratch_shapes=scratch,
        cost_estimate=pl.CostEstimate(flops=4 << 30, bytes_accessed=16 << 20, transcendentals=0),
        compiler_params=pltpu.CompilerParams(
            collective_id=0, has_side_effects=True, vmem_limit_bytes=48 << 20
        ),
    )(
        shell_motion,
        owner.reshape(own // LANES, LANES),
        stencil_slot,
        stencil_weight,
        prev_motion,
        node_offset,
        cell_split,
    )


def solution(mesh):
    return jax.shard_map(
        shards,
        mesh=mesh,
        in_specs=(
            P(None, ("struct", "fluid")),
            P(("struct", "fluid"), None),
            P(None, "struct", "fluid", None),
            P(None, "struct", "fluid", None),
            P(None, "struct", "fluid", None),
            P(None, "struct", "fluid", None),
            P("struct", "fluid", None),
        ),
        out_specs=P(None, "struct", "fluid", None),
        check_vma=False,
    )
```

profile of v0, /device:TPU:0, one launch (start us, length us, event | category | flops | bytes accessed | tf_op | source)
XLA Modules:
  0.0 42.7 jit_solution(754514071795987825)
XLA Ops:
  0.0 0.0 copy-start
  0.0 0.9 %copy-done = f32[3,8192]{1,0:T(4,128)S(1)} copy-done((f32[3,8192]{1,0:T(4,128)S(1)}, f32[3,8192]{1,0:T(4,128)}, u32[]{:S(2)}) %copy-start) | copy-done | bytes 98328
  0.9 0.0 copy-start.1
  0.9 0.8 %copy-done.1 = f32[3,2,8,256]{3,2,1,0:T(8,128)S(1)} copy-done((f32[3,2,8,256]{3,2,1,0:T(8,128)S(1)}, f32[3,2,8,256]{3,2,1,0:T(8,128)}, u32[]{:S(2)}) %copy-start.1) | copy-done | bytes 49176
  1.7 0.0 copy-start.2
  1.7 0.8 %copy-done.2 = f32[3,2,8,256]{3,2,1,0:T(8,128)S(1)} copy-done((f32[3,2,8,256]{3,2,1,0:T(8,128)S(1)}, f32[3,2,8,256]{3,2,1,0:T(8,128)}, u32[]{:S(2)}) %copy-start.2) | copy-done | bytes 49176
  2.5 0.0 copy-start.3
  2.5 0.8 %copy-done.3 = s32[8192,1]{0,1:T(1,128)S(1)} copy-done((s32[8192,1]{0,1:T(1,128)S(1)}, s32[8192,1]{0,1:T(1,128)}, u32[]{:S(2)}) %copy-start.3) | copy-done | bytes 32792
  3.3 0.0 copy-start.4
  3.3 0.8 %copy-done.4 = s32[4,2,8,128]{3,2,1,0:T(8,128)S(1)} copy-done((s32[4,2,8,128]{3,2,1,0:T(8,128)S(1)}, s32[4,2,8,128]{3,2,1,0:T(8,128)}, u32[]{:S(2)}) %copy-start.4) | copy-done | bytes 32792
  4.0 0.0 copy-start.5
  4.0 0.8 %copy-done.5 = f32[4,2,8,128]{3,2,1,0:T(8,128)S(1)} copy-done((f32[4,2,8,128]{3,2,1,0:T(8,128)S(1)}, f32[4,2,8,128]{3,2,1,0:T(8,128)}, u32[]{:S(2)}) %copy-start.5) | copy-done | bytes 32792
  4.8 0.0 copy-start.6
  4.8 0.7 %copy-done.6 = s32[2,8,256]{2,1,0:T(8,128)S(1)} copy-done((s32[2,8,256]{2,1,0:T(8,128)S(1)}, s32[2,8,256]{2,1,0:T(8,128)}, u32[]{:S(2)}) %copy-start.6) | copy-done | bytes 16408
  5.5 36.5 %shard_map.73 = f32[3,2,8,256]{3,2,1,0:T(8,128)S(1)} custom-call(f32[3,8192]{1,0:T(4,128)S(1)} %copy-done, s32[64,128]{1,0:T(8,128)S(1)} %bitcast.1, s32[4,2,8,128]{3,2,1,0:T(8,128)S(1)} %copy-done.4, f32[4,2,8,128]{3,2,1,0:T(8,128)S(1)} %copy-done.5, f32[3,2,8,256]{3,2,1,0:T(8,128)S(1)} %copy-done.1, f32[3,2,8,256]{3,2,1,0:T(8,128)S(1)} %copy-done.2, ...), custom_call_target="tpu_custom_call" | custom-call | flops 4294967296 | bytes 16777216 | tf_op jit(solution)/shard_map/pallas_call | solution.py:752
  42.0 0.6 %copy.9 = f32[3,2,8,256]{3,2,1,0:T(8,128)} copy(f32[3,2,8,256]{3,2,1,0:T(8,128)S(1)} %shard_map.73) | data formatting | bytes 98304
Async XLA Ops:
  0.0 0.9 %copy-start = (f32[3,8192]{1,0:T(4,128)S(1)}, f32[3,8192]{1,0:T(4,128)}, u32[]{:S(2)}) copy-start(f32[3,8192]{1,0:T(4,128)} %shell.1) | copy-start | bytes 294916
  0.9 0.8 %copy-start.1 = (f32[3,2,8,256]{3,2,1,0:T(8,128)S(1)}, f32[3,2,8,256]{3,2,1,0:T(8,128)}, u32[]{:S(2)}) copy-start(f32[3,2,8,256]{3,2,1,0:T(8,128)} %prev.1) | copy-start | bytes 147460
  1.7 0.8 %copy-start.2 = (f32[3,2,8,256]{3,2,1,0:T(8,128)S(1)}, f32[3,2,8,256]{3,2,1,0:T(8,128)}, u32[]{:S(2)}) copy-start(f32[3,2,8,256]{3,2,1,0:T(8,128)} %offset.1) | copy-start | bytes 147460
  2.5 0.8 %copy-start.3 = (s32[8192,1]{0,1:T(1,128)S(1)}, s32[8192,1]{0,1:T(1,128)}, u32[]{:S(2)}) copy-start(s32[8192,1]{0,1:T(1,128)} %param.8) | copy-start | bytes 98308
  3.3 0.8 %copy-start.4 = (s32[4,2,8,128]{3,2,1,0:T(8,128)S(1)}, s32[4,2,8,128]{3,2,1,0:T(8,128)}, u32[]{:S(2)}) copy-start(s32[4,2,8,128]{3,2,1,0:T(8,128)} %slot.1) | copy-start | bytes 98308
  4.0 0.8 %copy-start.5 = (f32[4,2,8,128]{3,2,1,0:T(8,128)S(1)}, f32[4,2,8,128]{3,2,1,0:T(8,128)}, u32[]{:S(2)}) copy-start(f32[4,2,8,128]{3,2,1,0:T(8,128)} %weight.1) | copy-start | bytes 98308
  4.8 0.7 %copy-start.6 = (s32[2,8,256]{2,1,0:T(8,128)S(1)}, s32[2,8,256]{2,1,0:T(8,128)}, u32[]{:S(2)}) copy-start(s32[2,8,256]{2,1,0:T(8,128)} %split.1) | copy-start | bytes 49156
where the time goes:
time: 43.2 us; the launch traced here: 42.7 us
  Pallas kernels  36.5 us (84%)
  local copies, waits for them, and re-layouts  6.11 us (14%)
    pallas_call x1, Pallas kernels, shards(): pl.pallas_call(functools.partial(window_kernel, (num_struct, num_fluid)),...  36.5 us
    unnamed x15, local copies, waits for them, and re-layouts  6.11 us

commit v1 on v0

v1 whole, which is shorter than its diff:
```python
import functools

import jax
import jax.numpy as jnp
from jax import lax
from jax.experimental import pallas as pl
from jax.experimental.pallas import tpu as pltpu
from jax.sharding import PartitionSpec as P

SWEEPS = 4
LANES = 128
LAMBDA_RATIO = 1.0
RELAX_FACTOR = 0.5
STEP_ORDERS = ((0, 1, 2), (0, 2, 1), (1, 0, 2), (1, 2, 0), (2, 0, 1), (2, 1, 0))
CORNERS = tuple((a, b, c) for a in (0, 1) for b in (0, 1) for c in (0, 1))
COLUMNS = 16
FIELDS = 8
ROW_STEP = 8
MESH = pl.DeviceIdType.MESH
BF16 = jnp.bfloat16
F32 = jnp.float32


def split_two(values):
    high = values.astype(BF16)
    low = (values - high.astype(F32)).astype(BF16)
    return high, low


def iota(shape, dim):
    return lax.broadcasted_iota(jnp.int32, shape, dim)


def swap_corners(corners, flip_y, flip_z):
    middle = {}
    for a, b, c in CORNERS:
        middle[a, b, c] = [
            jnp.where(flip_y, q, p) for p, q in zip(corners[a, b, c], corners[a, 1 - b, c])
        ]
    return {
        (a, b, c): [jnp.where(flip_z, q, p) for p, q in zip(middle[a, b, c], middle[a, b, 1 - c])]
        for a, b, c in CORNERS
    }


def paths():
    for order in STEP_ORDERS:
        position, path = [0, 0, 0], []
        for axis_id in order:
            position[axis_id] = 1
            path.append(tuple(position))
        yield path


def cross(p, q):
    return [p[1] * q[2] - p[2] * q[1], p[2] * q[0] - p[0] * q[2], p[0] * q[1] - p[1] * q[0]]


def add_to(table, key, vector):
    table[key] = [p + q for p, q in zip(table[key], vector)] if key in table else list(vector)


def cell_gradients(offsets, flip_y, flip_z):
    offsets = swap_corners(offsets, flip_y, flip_z)
    sign_y, sign_z = jnp.where(flip_y, -1.0, 1.0), jnp.where(flip_z, -1.0, 1.0)
    anchor = offsets[0, 0, 0]
    edges = {}
    for vertex in CORNERS[1:]:
        edge = [p - q for p, q in zip(offsets[vertex], anchor)]
        if vertex[0]:
            edge[0] = edge[0] + 1.0
        if vertex[1]:
            edge[1] = edge[1] + sign_y
        if vertex[2]:
            edge[2] = edge[2] + sign_z
        edges[vertex] = edge
    gradients, diagonal = [], {}
    for path in paths():
        one, two, three = [edges[v] for v in path]
        across = [cross(two, three), cross(three, one), cross(one, two)]
        volume = one[0] * across[0][0] + one[1] * across[0][1] + one[2] * across[0][2]
        inverse = 1.0 / volume
        grads = [[p * inverse for p in vector] for vector in across]
        gradients.append(grads)
        first = [-(grads[0][p] + grads[1][p] + grads[2][p]) for p in range(3)]
        for vertex, grad in zip([(0, 0, 0)] + path, [first] + grads):
            square = [p * p for p in grad]
            norm = square[0] + square[1] + square[2]
            add_to(diagonal, vertex, [(LAMBDA_RATIO + 1.0) * p + norm for p in square])
    return gradients, swap_corners(diagonal, flip_y, flip_z)


def cell_forces(gradients, motion, flip_y, flip_z):
    motion = swap_corners(motion, flip_y, flip_z)
    anchor = motion[0, 0, 0]
    moves = {v: [p - q for p, q in zip(motion[v], anchor)] for v in CORNERS[1:]}
    forces = {}
    for tet, path in enumerate(paths()):
        grads = [[gradients(tet, v, p) for p in range(3)] for v in range(3)]
        tensor = [
            [
                moves[path[0]][p] * grads[0][q]
                + moves[path[1]][p] * grads[1][q]
                + moves[path[2]][p] * grads[2][q]
                for q in range(3)
            ]
            for p in range(3)
        ]
        trace = LAMBDA_RATIO * (tensor[0][0] + tensor[1][1] + tensor[2][2])
        stress = [[None] * 3 for _ in range(3)]
        for p in range(3):
            stress[p][p] = tensor[p][p] + tensor[p][p] + trace
            for q in range(p):
                stress[p][q] = stress[q][p] = tensor[p][q] + tensor[q][p]
        for v in range(3):
            add_to(
                forces,
                path[v],
                [
                    stress[p][0] * grads[v][0] + stress[p][1] * grads[v][1] + stress[p][2] * grads[v][2]
                    for p in range(3)
                ],
            )
    first = None
    for vector in forces.values():
        first = vector if first is None else [p + q for p, q in zip(first, vector)]
    forces[0, 0, 0] = [-p for p in first]
    return swap_corners(forces, flip_y, flip_z)


def turn(x, shift, axis):
    shift %= x.shape[axis]
    return pltpu.roll(x, shift, axis) if shift else x


def float_codes(value):
    return value >= 1.5, (value == 1.0) | (value == 3.0)


def corners_of(low, high):
    corners = {}
    for b, row in ((0, low), (1, high)):
        for a in (0, 1):
            far = [turn(p, -a, 1) for p in row]
            corners[a, b, 0] = far
            corners[a, b, 1] = [turn(p, -1, 0) for p in far]
    return corners


def assemble_row(parts, b):
    near = [p + turn(q, 1, 0) for p, q in zip(parts[0, b, 0], parts[0, b, 1])]
    far = [p + turn(q, 1, 0) for p, q in zip(parts[1, b, 0], parts[1, b, 1])]
    return [p + turn(q, 1, 1) for p, q in zip(near, far)]


def one_hot(mask):
    return mask.astype(F32).astype(BF16)


def place_nodes(devices, capacity, own_ref, place_ref):
    rows = own_ref.shape[0]
    own = own_ref[...]
    upper = iota((LANES, LANES), 0) < iota((LANES, LANES), 1)
    prefix = jnp.concatenate([one_hot(upper), jnp.ones((LANES, LANES), BF16)], axis=0)
    lower = one_hot(iota((rows, rows), 1) < iota((rows, rows), 0))
    chunk = min(devices, 8)

    def ranks(step, place):
        masks = [own == step * chunk + o for o in range(chunk)]
        named = [one_hot(mask) for mask in masks]
        above = jnp.dot(lower, jnp.concatenate(named, axis=1), preferred_element_type=F32).astype(BF16)
        left = [
            jnp.concatenate([named[o], above[:, o * LANES : (o + 1) * LANES]], axis=1) for o in range(chunk)
        ]
        rank = jnp.dot(jnp.concatenate(left, axis=0), prefix, preferred_element_type=F32)
        for o in range(chunk):
            base = ((step * chunk + o) * capacity) * 1.0
            place = jnp.where(masks[o], rank[o * rows : (o + 1) * rows] + base, place)
        return place

    place = jnp.zeros((rows, LANES), F32)
    if devices <= 4 * chunk:
        for step in range(devices // chunk):
            place = ranks(step, place)
    else:
        place = lax.fori_loop(0, devices // chunk, ranks, place)
    place_ref[...] = place.astype(jnp.int32)


def pack_nodes(first, last, place_ref, val_ref, acc_ref):
    wide = 2 * LANES
    groups = acc_ref.shape[0] // 3
    pair = 16
    group_id = iota((groups, LANES), 0)
    lane_id = iota((wide, LANES), 0)

    def spread(step, carry):
        columns, parts = [], [[] for _ in range(6)]
        for u in range(ROW_STEP):
            row = step * ROW_STEP + u
            at = place_ref[pl.ds(row, 1), :]
            hit = one_hot(group_id == at // wide)
            columns.append(one_hot(lane_id == at % wide))
            for c in range(3):
                value = val_ref[pl.ds(c, 1), pl.ds(pl.multiple_of(row * LANES, LANES), LANES)]
                value = jnp.broadcast_to(value, (pair, LANES))
                high = value.astype(BF16)
                low = (value - high.astype(F32)).astype(BF16)
                for n, part in ((c, high), (3 + c, low)):
                    parts[n].append(hit * jnp.concatenate([part] * (groups // pair), axis=0))
        left = jnp.concatenate([jnp.concatenate(part, axis=1) for part in parts], axis=0)
        right = jnp.concatenate(columns, axis=1)
        product = lax.dot_general(left, right, (((1,), (1,)), ((), ())), preferred_element_type=F32)
        acc_ref[...] += product[: 3 * groups] + product[3 * groups :]
        return carry

    lax.fori_loop(first, last, spread, 0)


def window_kernel(
    counts,
    shell,
    owner,
    slot,
    weight,
    prev,
    offset,
    split,
    out,
    v_shell,
    v_owner,
    v_slot,
    v_weight,
    v_prev,
    v_offset,
    v_split,
    place,
    acc,
    packed,
    received,
    both,
    v_wall,
    tiles,
    near_in,
    wall_in,
    back_in,
    main_field,
    main_motion,
    main_force,
    main_grad,
    main_diag,
    edge_field,
    edge_motion,
    edge_grad,
    edge_diag,
    local_sem,
    near_send,
    near_recv,
    pack_send,
    pack_recv,
    wall_send,
    wall_recv,
    back_send,
    back_recv,
):
    num_struct, num_fluid = counts
    devices = num_struct * num_fluid
    s, f = lax.axis_index("struct"), lax.axis_index("fluid")
    me = s * num_fluid + f
    stencil, count_y, count_z, wall = slot.shape
    free = prev.shape[3] - wall
    nodes = count_y * count_z
    deep = 2 * count_z
    span = count_y * COLUMNS
    pitch = LANES // count_y
    share = free // num_struct
    rows_own = v_owner.shape[0]
    capacity = 2 * rows_own * LANES // devices
    pieces = capacity // LANES
    groups = devices * pieces
    far_wall = 2 * SWEEPS + SWEEPS + 1

    def peer(ds, df):
        return ((s + ds + num_struct) % num_struct, (f + df + num_fluid) % num_fluid)

    def remote(src, dst, send, recv, where):
        return pltpu.make_async_remote_copy(
            src_ref=src, dst_ref=dst, send_sem=send, recv_sem=recv, device_id=where, device_id_type=MESH
        )

    loads = [
        (owner, v_owner),
        (offset, v_offset),
        (split, v_split),
        (prev.at[:, :, :, pl.ds(wall, free)], v_prev),
        (shell, v_shell),
        (slot, v_slot),
        (weight, v_weight),
    ]
    loads = [pltpu.make_async_copy(a, b, local_sem.at[n]) for n, (a, b) in enumerate(loads)]
    for load in loads:
        load.start()

    barrier = pltpu.get_barrier_semaphore()

    def greet(d, carry):
        other = (me + d) % devices
        pl.semaphore_signal(
            barrier, inc=1, device_id=(other // num_fluid, other % num_fluid), device_id_type=MESH
        )
        return carry

    lax.fori_loop(1, devices, greet, 0)

    with jax.named_scope("place"):
        loads[0].wait()
        place_nodes(devices, capacity, v_owner, place)

    lane = iota((count_z, LANES), 1)
    with jax.named_scope("tiles"):
        for load in loads[1:4]:
            load.wait()
        slab = jnp.zeros((count_z, LANES), F32)
        for n in range(7):
            shifted = [[None] * count_y for _ in range(num_struct)]
            for j in range(count_y):
                if n < 3:
                    near, far = v_offset[n, j, :, :wall], v_offset[n, j, :, wall:]
                elif n == 3:
                    near, far = v_split[j, :, :wall].astype(F32), v_split[j, :, wall:].astype(F32)
                else:
                    near, far = jnp.zeros((count_z, LANES), F32), v_prev[n - 4, j]
                for q in range(num_struct):
                    begin = share * q - SWEEPS
                    line = far
                    if begin < 0:
                        line = jnp.where(lane >= LANES + begin, near, far)
                    if begin + pitch > LANES:
                        line = jnp.where(lane < begin + pitch - LANES, near, far)
                    shifted[q][j] = turn(line, pitch * j - begin, 1)
                if n < 4:
                    base = span * n + COLUMNS * j
                    low = turn(jnp.where(lane == LANES - 1, near, far), base + 1, 1)
                    high = turn(jnp.where(lane == 0, near, far), base + far_wall, 1)
                    slab = jnp.where((lane >= base) & (lane < base + 2 * SWEEPS), low, slab)
                    slab = jnp.where(
                        (lane >= base + 2 * SWEEPS) & (lane < base + COLUMNS), high, slab
                    )
            for q in range(num_struct):
                total = shifted[q][0]
                for j in range(1, count_y):
                    total = jnp.where(lane >= pitch * j, shifted[q][j], total)
                tiles[q, n] = total
        for q in range(num_struct):
            tiles[q, 7] = slab

    with jax.named_scope("barrier"):
        pl.semaphore_wait(barrier, devices - 1)

    around = [(r, df) for r in range(num_struct) for df in (0, -1, 1) if (r, df) != (0, 0)]

    def planes_of(df):
        return pl.ds(0, count_z) if df == 0 else pl.ds(0 if df > 0 else SWEEPS, SWEEPS)

    def near_copy(r, df):
        to = peer(-r, -df)
        return remote(
            tiles.at[to[0], :, planes_of(df)],
            near_in.at[r, 0 if df == 0 else 1, :, planes_of(df)],
            near_send.at[r, df + 1],
            near_recv.at[r, df + 1],
            to,
        )

    near_copies = [near_copy(r, df) for r, df in around]
    for copy in near_copies:
        copy.start()
    near_in[0, 0] = tiles[s]

    with jax.named_scope("pack"):
        acc[...] = jnp.zeros_like(acc)
        loads[4].wait()
        pack_nodes(0, rows_own // ROW_STEP, place, v_shell, acc)
    with jax.named_scope("relay"):
        pack_groups = groups // 2
        for o in range(devices):
            for c in range(3):
                for b in range(pieces):
                    m = o * pieces + b
                    packed[o, pl.ds(c * pieces + b, 1), :] = acc[
                        pl.ds(c * pack_groups + m // 2, 1), pl.ds((m % 2) * LANES, LANES)
                    ]

    with jax.named_scope("sendpack"):

        def send_pack(d, carry):
            other = (me + d) % devices
            remote(
                packed.at[other],
                received.at[me],
                pack_send,
                pack_recv,
                (other // num_fluid, other % num_fluid),
            ).start()
            return carry

        lax.fori_loop(1, devices, send_pack, 0)
        received[me] = packed[me]
    all_packs = remote(
        packed.at[pl.ds(0, devices - 1)],
        received.at[pl.ds(0, devices - 1)],
        pack_send,
        pack_recv,
        peer(1, 0),
    )

    lane_deep = iota((deep, LANES), 1)
    row_low = lane_deep < pitch
    column = lane_deep % pitch + share * s
    free_node = (column >= SWEEPS) & (column < free + SWEEPS)

    def main_row(read, r):
        following = (r + 1) % num_struct
        low = [read(r, c) for c in range(3)]
        high = [
            jnp.where(row_low, turn(p, pitch, 1), turn(read(following, c), pitch, 1))
            for c, p in enumerate(low)
        ]
        return corners_of(low, high), following

    def main_add(ref, r, following, parts):
        for c, (low, high) in enumerate(zip(assemble_row(parts, 0), assemble_row(parts, 1))):
            moved = turn(high, pitch, 1)
            ref[r, c] = ref[r, c] + low + jnp.where(row_low, 0.0, moved)
            ref[following, c] = ref[following, c] + jnp.where(row_low, moved, 0.0)

    def prepare_main():
        main_diag[...] = jnp.zeros_like(main_diag)
        for r in range(num_struct):
            for n in range(FIELDS):
                whole = jnp.concatenate([near_in[r, 0, n], near_in[r, 1, n]], axis=0)
                if n < 4:
                    main_field[r, n] = whole
                elif n < 7:
                    main_motion[r, n - 4] = whole
                else:
                    for m in range(4):
                        moved = turn(whole, span * (r - m), 1)
                        if r == 0:
                            edge_field[m] = moved
                        else:
                            edge_field[m] = jnp.where(lane_deep >= span * r, moved, edge_field[m])

        def row(r, carry):
            corners, following = main_row(lambda at, c: main_field[at, c], r)
            gradients, parts = cell_gradients(corners, *float_codes(main_field[r, 3]))
            for tet in range(6):
                for v in range(3):
                    for p in range(3):
                        main_grad[r, 9 * tet + 3 * v + p] = gradients[tet][v][p]
            main_add(main_diag, r, following, parts)
            return carry

        lax.fori_loop(0, num_struct, row, 0)

    def sweep_main(sweep, carry):
        main_force[...] = jnp.zeros_like(main_force)

        def row(r, inner):
            corners, following = main_row(lambda at, c: main_motion[at, c], r)
            parts = cell_forces(
                lambda tet, v, p: main_grad[r, 9 * tet + 3 * v + p],
                corners,
                *float_codes(main_field[r, 3]),
            )
            main_add(main_force, r, following, parts)
            return inner

        lax.fori_loop(0, num_struct, row, 0)
        for r in range(num_struct):
            for c in range(3):
                now = main_motion[r, c]
                change = RELAX_FACTOR * main_force[r, c] / main_diag[r, c]
                main_motion[r, c] = jnp.where(free_node, now - change, now)
        return carry

    def edge_corners(values):
        return corners_of(values, [turn(p, -COLUMNS, 1) for p in values])

    def edge_assemble(parts):
        low, high = assemble_row(parts, 0), assemble_row(parts, 1)
        return [p + turn(q, COLUMNS, 1) for p, q in zip(low, high)]

    def prepare_edge():
        gradients, parts = cell_gradients(
            edge_corners([edge_field[c] for c in range(3)]), *float_codes(edge_field[3])
        )
        for tet in range(6):
            for v in range(3):
                for p in range(3):
                    edge_grad[9 * tet + 3 * v + p] = gradients[tet][v][p]
        for c, value in enumerate(edge_assemble(parts)):
            edge_diag[c] = value

    def plane_points(ref, zero):
        row, at = iota((nodes, LANES), 0), iota((nodes, LANES), 1)
        within = row // count_z * (2 * count_z) + count_z - 1 - row % count_z
        total = None
        for t in range(stencil):
            whole = jnp.concatenate([ref[t, j] for j in range(count_y)], axis=0)
            for side in (0, 1):
                edge = wall - 1 if side == 0 else 0
                spread = jnp.broadcast_to(whole[:, edge : edge + 1], (nodes, LANES))
                part = jnp.where(at == 2 * nodes * t + count_z * side + within, spread, zero)
                total = part if total is None else total + part
        return jnp.sum(total, axis=0, keepdims=True)

    with jax.named_scope("waitnear"):
        for copy in near_copies:
            copy.wait_recv()
    with jax.named_scope("prepmain"):
        prepare_main()
    with jax.named_scope("sweeps"):
        lax.fori_loop(0, SWEEPS, sweep_main, 0)

    def back_copy(r):
        at = (s + r) % num_struct
        return remote(
            main_motion.at[r, :, pl.ds(0, count_z)],
            back_in.at[s],
            back_send.at[r],
            back_recv.at[s],
            peer(r, 0),
        ), remote(
            main_motion.at[r, :, pl.ds(0, count_z)],
            back_in.at[at],
            back_send.at[r],
            back_recv.at[at],
            peer(r, 0),
        )

    back_copies = [back_copy(r) for r in range(1, num_struct)]
    for copy, _ in back_copies:
        copy.start()
    back_in[s] = main_motion[0, :, :count_z, :]
    with jax.named_scope("prepedge"):
        prepare_edge()
    with jax.named_scope("points"):
        loads[5].wait()
        loads[6].wait()
        plane_slot, plane_weight = plane_points(v_slot, 0), plane_points(v_weight, 0.0)

    with jax.named_scope("waitpack"):
        all_packs.wait_recv()

    with jax.named_scope("table"):
        for c in range(3):
            whole = jnp.concatenate(
                [received[o, pl.ds(c * pieces, pieces), :] for o in range(devices)], axis=0
            )
            high, low = split_two(whole)
            both[pl.ds(c * groups, groups), :LANES] = high
            both[pl.ds(c * groups, groups), LANES:] = low

    with jax.named_scope("planes"):
        pick = one_hot(iota((LANES, LANES), 0) == plane_slot % LANES)
        found = jnp.dot(both[...], jnp.concatenate([pick, pick], axis=0), preferred_element_type=F32)
        scaled = jnp.where(iota((groups, LANES), 0) == plane_slot // LANES, plane_weight, 0.0)
        tile = jnp.zeros((count_z, LANES), F32)
        for c in range(3):
            line = jnp.sum(found[c * groups : (c + 1) * groups] * scaled, axis=0, keepdims=True)
            period = LANES // 2
            while period >= 2 * nodes:
                line = line + turn(line, period, 1)
                period //= 2
            spread = pltpu.roll(jnp.broadcast_to(line, (count_z, LANES)), 0, 1, stride=1, stride_axis=0)
            tile = jnp.where((lane >= span * c) & (lane < span * (c + 1)), spread, tile)
        wall_in[0, 0] = tile

    def wall_copy(r, df):
        return remote(
            wall_in.at[0, 0, planes_of(df)],
            wall_in.at[r, 0 if df == 0 else 1, planes_of(df)],
            wall_send.at[r, df + 1],
            wall_recv.at[r, df + 1],
            peer(-r, -df),
        )

    wall_copies = [wall_copy(r, df) for r, df in around]
    for copy in wall_copies:
        copy.start()

    wide = 2 * LANES
    lane_id = iota((LANES, wide), 0)
    group_id = iota((groups, wide), 0)

    def pair(step, carry):
        j, k = 2 * step // count_z, 2 * step % count_z
        sums = [None] * 3
        for t in range(stencil):
            at = jnp.concatenate(
                [v_slot[t, j, pl.ds(k, 1), :], v_slot[t, j, pl.ds(k + 1, 1), :]], axis=1
            )
            by = jnp.concatenate(
                [v_weight[t, j, pl.ds(k, 1), :], v_weight[t, j, pl.ds(k + 1, 1), :]], axis=1
            )
            choose = one_hot(lane_id == at % LANES)
            values = jnp.dot(
                both[...], jnp.concatenate([choose, choose], axis=0), preferred_element_type=F32
            )
            factor = jnp.where(group_id == at // LANES, by, 0.0)
            for c in range(3):
                term = values[c * groups : (c + 1) * groups] * factor
                sums[c] = term if sums[c] is None else sums[c] + term
        for c in range(3):
            line = jnp.sum(sums[c], axis=0, keepdims=True)
            v_wall[c, pl.ds(2 * step, 1), :] = line[:, :LANES]
            v_wall[c, pl.ds(2 * step + 1, 1), :] = line[:, LANES:]
        return carry

    with jax.named_scope("wall"):
        lax.fori_loop(0, nodes // 2, pair, 0)

    with jax.named_scope("waitwall"):
        for copy in wall_copies:
            copy.wait_recv()
    with jax.named_scope("edgeinit"):
        within = lane_deep % COLUMNS
        inner = ((within >= 1) & (within <= SWEEPS)) | ((within > 2 * SWEEPS) & (within < far_wall))
        arrived = [jnp.concatenate([wall_in[r, 0], wall_in[r, 1]], axis=0) for r in range(num_struct)]
        for c in range(3):
            total = jnp.zeros((deep, LANES), F32)
            for r in range(num_struct):
                here = lane_deep // span == r
                shift = span * (r - c) - (count_z - 1)
                total = jnp.where(here & (within == 0), turn(arrived[r], shift, 1), total)
                shift = shift - count_z + far_wall
                total = jnp.where(here & (within == far_wall), turn(arrived[r], shift, 1), total)
            edge_motion[c] = total

    def sweep_edge(step, carry):
        parts = cell_forces(
            lambda tet, v, p: edge_grad[9 * tet + 3 * v + p],
            edge_corners([edge_motion[c] for c in range(3)]),
            *float_codes(edge_field[3]),
        )
        for c, value in enumerate(edge_assemble(parts)):
            now = edge_motion[c]
            edge_motion[c] = jnp.where(inner, now - RELAX_FACTOR * value / edge_diag[c], now)
        return carry

    with jax.named_scope("sweepedge"):
        lax.fori_loop(0, SWEEPS, sweep_edge, 0)

    with jax.named_scope("waitback"):
        for _, copy in back_copies:
            copy.wait_recv()
    with jax.named_scope("outs"):
        for c in range(3):
            for j in range(count_y):
                out[c, j, :, :wall] = v_wall[c, pl.ds(j * count_z, count_z), :]
                total = None
                for q in range(num_struct):
                    moved = turn(back_in[q, c], share * q - pitch * j - SWEEPS, 1)
                    total = moved if total is None else jnp.where(lane >= share * q, moved, total)
                delta = edge_motion[c, :count_z, :]
                low = turn(delta, -1 - COLUMNS * j, 1)
                high = turn(delta, free - far_wall - COLUMNS * j, 1)
                change = jnp.where(lane < SWEEPS, low, jnp.where(lane >= free - SWEEPS, high, 0.0))
                out[c, j, :, wall:] = total + change

    with jax.named_scope("waitsend"):
        for copy in near_copies + wall_copies + [copy for copy, _ in back_copies]:
            copy.wait_send()
        all_packs.wait_send()


def shards(shell_motion, owner, stencil_slot, stencil_weight, prev_motion, node_offset, cell_split):
    num_struct, num_fluid = lax.axis_size("struct"), lax.axis_size("fluid")
    devices = num_struct * num_fluid
    own = shell_motion.shape[1]
    pieces = 2 * own // devices // LANES
    groups = devices * pieces
    stencil, count_y, count_z, wall = stencil_slot.shape
    total_x = prev_motion.shape[3]
    free = total_x - wall
    nodes, deep = count_y * count_z, 2 * count_z
    assert wall == free == LANES and count_z == 2 * SWEEPS == 8 and num_struct >= 2 and num_fluid >= 3
    assert num_struct * count_y * COLUMNS == LANES and 2 * stencil * nodes == LANES
    assert free // num_struct + 2 * SWEEPS <= LANES // count_y
    vmem, dma = pltpu.VMEM, pltpu.SemaphoreType.DMA
    scratch = [
        vmem((3, own), F32),
        vmem((own // LANES, LANES), jnp.int32),
        vmem((stencil, count_y, count_z, wall), jnp.int32),
        vmem((stencil, count_y, count_z, wall), F32),
        vmem((3, count_y, count_z, free), F32),
        vmem((3, count_y, count_z, total_x), F32),
        vmem((count_y, count_z, total_x), jnp.int32),
        vmem((own // LANES, LANES), jnp.int32),
        vmem((3 * groups // 2, 2 * LANES), F32),
        vmem((devices, 3 * pieces, LANES), F32),
        vmem((devices, 3 * pieces, LANES), F32),
        vmem((3 * groups, 2 * LANES), BF16),
        vmem((3, nodes, wall), F32),
        vmem((num_struct, FIELDS, count_z, LANES), F32),
        vmem((num_struct, 2, FIELDS, count_z, LANES), F32),
        vmem((num_struct, 2, count_z, LANES), F32),
        vmem((num_struct, 3, count_z, LANES), F32),
        vmem((num_struct, 4, deep, LANES), F32),
        vmem((num_struct, 3, deep, LANES), F32),
        vmem((num_struct, 3, deep, LANES), F32),
        vmem((num_struct, 54, deep, LANES), F32),
        vmem((num_struct, 3, deep, LANES), F32),
        vmem((4, deep, LANES), F32),
        vmem((3, deep, LANES), F32),
        vmem((54, deep, LANES), F32),
        vmem((3, deep, LANES), F32),
        dma((7,)),
        dma((num_struct, 3)),
        dma((num_struct, 3)),
        dma,
        dma,
        dma((num_struct, 3)),
        dma((num_struct, 3)),
        dma((num_struct,)),
        dma((num_struct,)),
    ]
    return pl.pallas_call(
        functools.partial(window_kernel, (num_struct, num_fluid)),
        out_shape=pltpu.VMEM(prev_motion.shape, F32),
        in_specs=[pl.BlockSpec(memory_space=pltpu.HBM)] * 7,
        out_specs=pl.BlockSpec(memory_space=pltpu.VMEM),
        scratch_shapes=scratch,
        cost_estimate=pl.CostEstimate(flops=4 << 30, bytes_accessed=16 << 20, transcendentals=0),
        compiler_params=pltpu.CompilerParams(
            collective_id=0, has_side_effects=True, vmem_limit_bytes=67043328 - (1 << 17)
        ),
    )(
        shell_motion,
        owner.reshape(own // LANES, LANES),
        stencil_slot,
        stencil_weight,
        prev_motion,
        node_offset,
        cell_split,
    )


def solution(mesh):
    return jax.shard_map(
        shards,
        mesh=mesh,
        in_specs=(
            P(None, ("struct", "fluid")),
            P(("struct", "fluid"), None),
            P(None, "struct", "fluid", None),
            P(None, "struct", "fluid", None),
            P(None, "struct", "fluid", None),
            P(None, "struct", "fluid", None),
            P("struct", "fluid", None),
        ),
        out_specs=P(None, "struct", "fluid", None),
        check_vma=False,
    )
```

time: 43.2 us -> 28.7 us (0.66)
  Pallas kernels: 36.5 us -> 27.9 us
  local copies, waits for them, and re-layouts: 6.11 us -> 0.62 us
    pallas_call x1, Pallas kernels: 36.5 us -> 27.9 us  [shards(): pl.pallas_call(functools.partial(window_kernel, (num_struct, num_fluid)),...]
    unnamed x15 -> x1, local copies, waits for them, and re-layouts: 6.11 us -> 0.62 us
where the time goes in v1:
time: 28.7 us; the launch traced here: 28.5 us
  Pallas kernels  27.9 us (97%)
  local copies, waits for them, and re-layouts  0.62 us (2%)
    pallas_call x1, Pallas kernels, shards(): pl.pallas_call(functools.partial(window_kernel, (num_struct, num_fluid)),...  27.9 us
    unnamed x1, local copies, waits for them, and re-layouts  0.62 us

profile of v1, /device:TPU:0, one launch (start us, length us, event | category | flops | bytes accessed | tf_op | source)
XLA Modules:
  0.0 28.5 jit_solution(17183172324681597723)
XLA Ops:
  0.0 27.9 %shard_map.73 = f32[3,2,8,256]{3,2,1,0:T(8,128)S(1)} custom-call(f32[3,8192]{1,0:T(4,128)} %shell.1, s32[64,128]{1,0:T(8,128)} %bitcast.1, s32[4,2,8,128]{3,2,1,0:T(8,128)} %slot.1, f32[4,2,8,128]{3,2,1,0:T(8,128)} %weight.1, f32[3,2,8,256]{3,2,1,0:T(8,128)} %prev.1, f32[3,2,8,256]{3,2,1,0:T(8,128)} %offset.1, s32[2,8,256]{2,1,0:T(8,128)} %split.1), custom_call_target="tpu_custom_call" | custom-call | flops 4294967296 | bytes 16777216 | tf_op jit(solution)/shard_map/pallas_call | solution.py:729
  27.9 0.6 %copy.9 = f32[3,2,8,256]{3,2,1,0:T(8,128)} copy(f32[3,2,8,256]{3,2,1,0:T(8,128)S(1)} %shard_map.73) | data formatting | bytes 98304

commit v2 on v1

--- a/solution.py
+++ b/solution.py
@@ -15,7 +15,9 @@
 CORNERS = tuple((a, b, c) for a in (0, 1) for b in (0, 1) for c in (0, 1))
 COLUMNS = 16
 FIELDS = 8
-ROW_STEP = 8
+ROW_STEP = 16
+WALL_STEP = 4
+EARLY_SWEEPS = 2
 MESH = pl.DeviceIdType.MESH
 BF16 = jnp.bfloat16
 F32 = jnp.float32
@@ -60,72 +62,130 @@
     table[key] = [p + q for p, q in zip(table[key], vector)] if key in table else list(vector)
 
 
-def cell_gradients(offsets, flip_y, flip_z):
-    offsets = swap_corners(offsets, flip_y, flip_z)
-    sign_y, sign_z = jnp.where(flip_y, -1.0, 1.0), jnp.where(flip_z, -1.0, 1.0)
+RING = ((1, 0, 0), (1, 1, 0), (0, 1, 0), (0, 1, 1), (0, 0, 1), (1, 0, 1))
+TOP = (1, 1, 1)
+
+
+def ring_tets():
+    order = [tuple(path) for path in paths()]
+    for k in range(6):
+        one, two = RING[k], RING[(k + 1) % 6]
+        if sum(one) > sum(two):
+            one, two = two, one
+        yield order.index((one, two, TOP)), (one, two, TOP)
+
+
+def slot_of(corner, p):
+    return 3 * CORNERS.index(corner) + p
+
+
+def halves(ref):
+    rows = ref.shape[1]
+    return [pl.ds(h, 8) for h in range(0, rows, 8)]
+
+
+def finish(sums, k, give):
+    done = []
+    if k > 0:
+        done.append(RING[k])
+    if k == 5:
+        done += [RING[0], TOP]
+    for corner in done:
+        give(corner, sums.pop(corner))
+
+
+def open_gradients(offsets, flips, work):
+    offsets = swap_corners(offsets, *flips)
+    signs = [None] + [jnp.where(flip, -1.0, 1.0) for flip in flips]
     anchor = offsets[0, 0, 0]
-    edges = {}
     for vertex in CORNERS[1:]:
-        edge = [p - q for p, q in zip(offsets[vertex], anchor)]
-        if vertex[0]:
-            edge[0] = edge[0] + 1.0
-        if vertex[1]:
-            edge[1] = edge[1] + sign_y
-        if vertex[2]:
-            edge[2] = edge[2] + sign_z
-        edges[vertex] = edge
-    gradients, diagonal = [], {}
-    for path in paths():
-        one, two, three = [edges[v] for v in path]
-        across = [cross(two, three), cross(three, one), cross(one, two)]
-        volume = one[0] * across[0][0] + one[1] * across[0][1] + one[2] * across[0][2]
-        inverse = 1.0 / volume
-        grads = [[p * inverse for p in vector] for vector in across]
-        gradients.append(grads)
-        first = [-(grads[0][p] + grads[1][p] + grads[2][p]) for p in range(3)]
-        for vertex, grad in zip([(0, 0, 0)] + path, [first] + grads):
-            square = [p * p for p in grad]
-            norm = square[0] + square[1] + square[2]
-            add_to(diagonal, vertex, [(LAMBDA_RATIO + 1.0) * p + norm for p in square])
-    return gradients, swap_corners(diagonal, flip_y, flip_z)
-
-
-def cell_forces(gradients, motion, flip_y, flip_z):
-    motion = swap_corners(motion, flip_y, flip_z)
+        for p in range(3):
+            edge = offsets[vertex][p] - anchor[p]
+            if vertex[p]:
+                edge = edge + (signs[p] if p else 1.0)
+            work[0, slot_of(vertex, p)] = edge
+
+
+def fill_gradients(work, put):
+    for rows in halves(work.at[0]):
+        sums = {}
+        for k, (tet, path) in enumerate(ring_tets()):
+            one, two, three = [[work[0, slot_of(v, p), rows] for p in range(3)] for v in path]
+            across = [cross(two, three), cross(three, one), cross(one, two)]
+            inverse = 1.0 / (one[0] * across[0][0] + one[1] * across[0][1] + one[2] * across[0][2])
+            grads = [[p * inverse for p in vector] for vector in across]
+            for v in range(3):
+                for p in range(3):
+                    put(9 * tet + 3 * v + p, rows, grads[v][p])
+            first = [grads[0][p] + grads[1][p] + grads[2][p] for p in range(3)]
+            for vertex, grad in zip(((0, 0, 0),) + path, [first] + grads):
+                square = [p * p for p in grad]
+                norm = square[0] + square[1] + square[2]
+                add_to(sums, vertex, [(LAMBDA_RATIO + 1.0) * p + norm for p in square])
+
+            def give(corner, vector):
+                for p in range(3):
+                    work[1, slot_of(corner, p), rows] = vector[p]
+
+            finish(sums, k, give)
+        give((0, 0, 0), sums[0, 0, 0])
+
+
+def close_cells(work, flips):
+    parts = swap_corners({v: [work[1, slot_of(v, p)] for p in range(3)] for v in CORNERS}, *flips)
+    return {
+        (a, b): [p + turn(q, 1, 0) for p, q in zip(parts[a, b, 0], parts[a, b, 1])]
+        for a in (0, 1)
+        for b in (0, 1)
+    }
+
+
+def open_forces(motion, flips, work):
+    motion = swap_corners(motion, *flips)
     anchor = motion[0, 0, 0]
-    moves = {v: [p - q for p, q in zip(motion[v], anchor)] for v in CORNERS[1:]}
-    forces = {}
-    for tet, path in enumerate(paths()):
-        grads = [[gradients(tet, v, p) for p in range(3)] for v in range(3)]
-        tensor = [
-            [
-                moves[path[0]][p] * grads[0][q]
-                + moves[path[1]][p] * grads[1][q]
-                + moves[path[2]][p] * grads[2][q]
-                for q in range(3)
+    for vertex in CORNERS[1:]:
+        for p in range(3):
+            work[0, slot_of(vertex, p)] = motion[vertex][p] - anchor[p]
+
+
+def fill_forces(get, work):
+    for rows in halves(work.at[0]):
+        sums, total = {}, [None]
+        top = [work[0, slot_of(TOP, p), rows] for p in range(3)]
+        for k, (tet, path) in enumerate(ring_tets()):
+            grads = [[get(9 * tet + 3 * v + p, rows) for p in range(3)] for v in range(3)]
+            moves = [[work[0, slot_of(v, p), rows] for p in range(3)] for v in path[:2]] + [top]
+            tensor = [
+                [
+                    moves[0][p] * grads[0][q] + moves[1][p] * grads[1][q] + moves[2][p] * grads[2][q]
+                    for q in range(3)
+                ]
+                for p in range(3)
             ]
-            for p in range(3)
-        ]
-        trace = LAMBDA_RATIO * (tensor[0][0] + tensor[1][1] + tensor[2][2])
-        stress = [[None] * 3 for _ in range(3)]
+            trace = LAMBDA_RATIO * (tensor[0][0] + tensor[1][1] + tensor[2][2])
+            stress = [[None] * 3 for _ in range(3)]
+            for p in range(3):
+                stress[p][p] = tensor[p][p] + tensor[p][p] + trace
+                for q in range(p):
+                    stress[p][q] = stress[q][p] = tensor[p][q] + tensor[q][p]
+            for v in range(3):
+                add_to(
+                    sums,
+                    path[v],
+                    [
+                        stress[p][0] * grads[v][0] + stress[p][1] * grads[v][1] + stress[p][2] * grads[v][2]
+                        for p in range(3)
+                    ],
+                )
+
+            def give(corner, vector):
+                for p in range(3):
+                    work[1, slot_of(corner, p), rows] = vector[p]
+                total[0] = vector if total[0] is None else [p + q for p, q in zip(total[0], vector)]
+
+            finish(sums, k, give)
         for p in range(3):
-            stress[p][p] = tensor[p][p] + tensor[p][p] + trace
-            for q in range(p):
-                stress[p][q] = stress[q][p] = tensor[p][q] + tensor[q][p]
-        for v in range(3):
-            add_to(
-                forces,
-                path[v],
-                [
-                    stress[p][0] * grads[v][0] + stress[p][1] * grads[v][1] + stress[p][2] * grads[v][2]
-                    for p in range(3)
-                ],
-            )
-    first = None
-    for vector in forces.values():
-        first = vector if first is None else [p + q for p, q in zip(first, vector)]
-    forces[0, 0, 0] = [-p for p in first]
-    return swap_corners(forces, flip_y, flip_z)
+            work[1, p, rows] = -total[0][p]
 
 
 def turn(x, shift, axis):
@@ -137,20 +197,12 @@
     return value >= 1.5, (value == 1.0) | (value == 3.0)
 
 
-def corners_of(low, high):
+def with_planes(edges):
     corners = {}
-    for b, row in ((0, low), (1, high)):
-        for a in (0, 1):
-            far = [turn(p, -a, 1) for p in row]
-            corners[a, b, 0] = far
-            corners[a, b, 1] = [turn(p, -1, 0) for p in far]
+    for (a, b), values in edges.items():
+        corners[a, b, 0] = values
+        corners[a, b, 1] = [turn(p, -1, 0) for p in values]
     return corners
-
-
-def assemble_row(parts, b):
-    near = [p + turn(q, 1, 0) for p, q in zip(parts[0, b, 0], parts[0, b, 1])]
-    far = [p + turn(q, 1, 0) for p, q in zip(parts[1, b, 0], parts[1, b, 1])]
-    return [p + turn(q, 1, 1) for p, q in zip(near, far)]
 
 
 def one_hot(mask):
@@ -246,13 +298,13 @@
     back_in,
     main_field,
     main_motion,
-    main_force,
     main_grad,
-    main_diag,
+    main_scale,
     edge_field,
     edge_motion,
     edge_grad,
-    edge_diag,
+    edge_scale,
+    work,
     local_sem,
     near_send,
     near_recv,
@@ -366,16 +418,17 @@
         to = peer(-r, -df)
         return remote(
             tiles.at[to[0], :, planes_of(df)],
-            near_in.at[r, 0 if df == 0 else 1, :, planes_of(df)],
-            near_send.at[r, df + 1],
-            near_recv.at[r, df + 1],
+            near_in.at[2 * r + (df != 0), :, planes_of(df)],
+            near_send,
+            near_recv,
             to,
         )
 
-    near_copies = [near_copy(r, df) for r, df in around]
-    for copy in near_copies:
-        copy.start()
-    near_in[0, 0] = tiles[s]
+    for r, df in around:
+        near_copy(r, df).start()
+    others = pl.ds(1, 2 * num_struct - 1)
+    all_near = remote(near_in.at[others], near_in.at[others], near_send, near_recv, peer(1, 0))
+    near_in[0] = tiles[s]
 
     with jax.named_scope("pack"):
         acc[...] = jnp.zeros_like(acc)
@@ -417,28 +470,39 @@
     lane_deep = iota((deep, LANES), 1)
     row_low = lane_deep < pitch
     column = lane_deep % pitch + share * s
+    within = lane_deep % COLUMNS
+    inner = ((within >= 1) & (within <= SWEEPS)) | ((within > 2 * SWEEPS) & (within < far_wall))
     free_node = (column >= SWEEPS) & (column < free + SWEEPS)
 
-    def main_row(read, r):
-        following = (r + 1) % num_struct
-        low = [read(r, c) for c in range(3)]
-        high = [
-            jnp.where(row_low, turn(p, pitch, 1), turn(read(following, c), pitch, 1))
-            for c, p in enumerate(low)
-        ]
-        return corners_of(low, high), following
-
-    def main_add(ref, r, following, parts):
-        for c, (low, high) in enumerate(zip(assemble_row(parts, 0), assemble_row(parts, 1))):
-            moved = turn(high, pitch, 1)
-            ref[r, c] = ref[r, c] + low + jnp.where(row_low, 0.0, moved)
-            ref[following, c] = ref[following, c] + jnp.where(row_low, moved, 0.0)
+    def main_corners(read):
+        values = [[read(r, c) for c in range(3)] for r in range(num_struct)]
+        moved = [[[turn(p, n, 1) for p in row] for row in values] for n in (-1, pitch, pitch - 1)]
+        for r in range(num_struct):
+            high = [
+                [jnp.where(row_low, p, q) for p, q in zip(moved[n][r], moved[n][(r + 1) % num_struct])]
+                for n in (1, 2)
+            ]
+            yield r, with_planes(
+                {(0, 0): values[r], (1, 0): moved[0][r], (0, 1): high[0], (1, 1): high[1]}
+            )
+
+    def main_sums():
+        lows, highs = [], []
+        for r in range(num_struct):
+            ends = close_cells(work.at[r], float_codes(main_field[r, 3]))
+            lows.append([p + turn(q, 1, 1) for p, q in zip(ends[0, 0], ends[1, 0])])
+            highs.append(
+                [turn(p, pitch, 1) + turn(q, pitch + 1, 1) for p, q in zip(ends[0, 1], ends[1, 1])]
+            )
+        for r in range(num_struct):
+            yield r, [
+                p + jnp.where(row_low, before, now) for p, before, now in zip(lows[r], highs[r - 1], highs[r])
+            ]
 
     def prepare_main():
-        main_diag[...] = jnp.zeros_like(main_diag)
         for r in range(num_struct):
             for n in range(FIELDS):
-                whole = jnp.concatenate([near_in[r, 0, n], near_in[r, 1, n]], axis=0)
+                whole = jnp.concatenate([near_in[2 * r, n], near_in[2 * r + 1, n]], axis=0)
                 if n < 4:
                     main_field[r, n] = whole
                 elif n < 7:
@@ -451,56 +515,52 @@
                         else:
                             edge_field[m] = jnp.where(lane_deep >= span * r, moved, edge_field[m])
 
+        for r, corners in main_corners(lambda at, c: main_field[at, c]):
+            open_gradients(corners, float_codes(main_field[r, 3]), work.at[r])
+
         def row(r, carry):
-            corners, following = main_row(lambda at, c: main_field[at, c], r)
-            gradients, parts = cell_gradients(corners, *float_codes(main_field[r, 3]))
-            for tet in range(6):
-                for v in range(3):
-                    for p in range(3):
-                        main_grad[r, 9 * tet + 3 * v + p] = gradients[tet][v][p]
-            main_add(main_diag, r, following, parts)
+            def put(n, rows, value):
+                main_grad[r, n, rows] = value
+
+            fill_gradients(work.at[r], put)
             return carry
 
         lax.fori_loop(0, num_struct, row, 0)
+        for r, values in main_sums():
+            for c in range(3):
+                main_scale[r, c] = jnp.where(free_node, RELAX_FACTOR / values[c], 0.0)
 
     def sweep_main(sweep, carry):
-        main_force[...] = jnp.zeros_like(main_force)
-
-        def row(r, inner):
-            corners, following = main_row(lambda at, c: main_motion[at, c], r)
-            parts = cell_forces(
-                lambda tet, v, p: main_grad[r, 9 * tet + 3 * v + p],
-                corners,
-                *float_codes(main_field[r, 3]),
-            )
-            main_add(main_force, r, following, parts)
-            return inner
-
-        lax.fori_loop(0, num_struct, row, 0)
+        for r, corners in main_corners(lambda at, c: main_motion[at, c]):
+            open_forces(corners, float_codes(main_field[r, 3]), work.at[r])
+
         for r in range(num_struct):
+            fill_forces(lambda n, rows: main_grad[r, n, rows], work.at[r])
+        for r, values in main_sums():
             for c in range(3):
-                now = main_motion[r, c]
-                change = RELAX_FACTOR * main_force[r, c] / main_diag[r, c]
-                main_motion[r, c] = jnp.where(free_node, now - change, now)
+                main_motion[r, c] = main_motion[r, c] - main_scale[r, c] * values[c]
         return carry
 
-    def edge_corners(values):
-        return corners_of(values, [turn(p, -COLUMNS, 1) for p in values])
-
-    def edge_assemble(parts):
-        low, high = assemble_row(parts, 0), assemble_row(parts, 1)
-        return [p + turn(q, COLUMNS, 1) for p, q in zip(low, high)]
+    def edge_corners(read):
+        values = [read(c) for c in range(3)]
+        return with_planes(
+            {(a, b): [turn(p, -a - COLUMNS * b, 1) for p in values] for a in (0, 1) for b in (0, 1)}
+        )
+
+    def edge_sums():
+        ends = close_cells(work.at[0], float_codes(edge_field[3]))
+        moved = [[turn(p, a + COLUMNS * b, 1) for p in ends[a, b]] for a in (0, 1) for b in (0, 1)]
+        return [(p + q) + (u + v) for p, q, u, v in zip(*moved)]
 
     def prepare_edge():
-        gradients, parts = cell_gradients(
-            edge_corners([edge_field[c] for c in range(3)]), *float_codes(edge_field[3])
-        )
-        for tet in range(6):
-            for v in range(3):
-                for p in range(3):
-                    edge_grad[9 * tet + 3 * v + p] = gradients[tet][v][p]
-        for c, value in enumerate(edge_assemble(parts)):
-            edge_diag[c] = value
+        open_gradients(edge_corners(lambda c: edge_field[c]), float_codes(edge_field[3]), work.at[0])
+
+        def put(n, rows, value):
+            edge_grad[n, rows] = value
+
+        fill_gradients(work.at[0], put)
+        for c, value in enumerate(edge_sums()):
+            edge_scale[c] = jnp.where(inner, RELAX_FACTOR / value, 0.0)
 
     def plane_points(ref, zero):
         row, at = iota((nodes, LANES), 0), iota((nodes, LANES), 1)
@@ -516,33 +576,11 @@
         return jnp.sum(total, axis=0, keepdims=True)
 
     with jax.named_scope("waitnear"):
-        for copy in near_copies:
-            copy.wait_recv()
+        all_near.wait_recv()
     with jax.named_scope("prepmain"):
         prepare_main()
     with jax.named_scope("sweeps"):
-        lax.fori_loop(0, SWEEPS, sweep_main, 0)
-
-    def back_copy(r):
-        at = (s + r) % num_struct
-        return remote(
-            main_motion.at[r, :, pl.ds(0, count_z)],
-            back_in.at[s],
-            back_send.at[r],
-            back_recv.at[s],
-            peer(r, 0),
-        ), remote(
-            main_motion.at[r, :, pl.ds(0, count_z)],
-            back_in.at[at],
-            back_send.at[r],
-            back_recv.at[at],
-            peer(r, 0),
-        )
-
-    back_copies = [back_copy(r) for r in range(1, num_struct)]
-    for copy, _ in back_copies:
-        copy.start()
-    back_in[s] = main_motion[0, :, :count_z, :]
+        lax.fori_loop(0, EARLY_SWEEPS, sweep_main, 0)
     with jax.named_scope("prepedge"):
         prepare_edge()
     with jax.named_scope("points"):
@@ -575,26 +613,39 @@
                 period //= 2
             spread = pltpu.roll(jnp.broadcast_to(line, (count_z, LANES)), 0, 1, stride=1, stride_axis=0)
             tile = jnp.where((lane >= span * c) & (lane < span * (c + 1)), spread, tile)
-        wall_in[0, 0] = tile
+        wall_in[0] = tile
 
     def wall_copy(r, df):
         return remote(
-            wall_in.at[0, 0, planes_of(df)],
-            wall_in.at[r, 0 if df == 0 else 1, planes_of(df)],
-            wall_send.at[r, df + 1],
-            wall_recv.at[r, df + 1],
+            wall_in.at[0, planes_of(df)],
+            wall_in.at[2 * r + (df != 0), planes_of(df)],
+            wall_send,
+            wall_recv,
             peer(-r, -df),
         )
 
-    wall_copies = [wall_copy(r, df) for r, df in around]
-    for copy in wall_copies:
-        copy.start()
-
+    for r, df in around:
+        wall_copy(r, df).start()
+    all_walls = remote(wall_in.at[others], wall_in.at[others], wall_send, wall_recv, peer(1, 0))
+
+    with jax.named_scope("latesweeps"):
+        lax.fori_loop(EARLY_SWEEPS, SWEEPS, sweep_main, 0)
+
+    def send_back():
+        for r in range(1, num_struct):
+            remote(
+                main_motion.at[r, :, pl.ds(0, count_z)], back_in.at[s], back_send, back_recv, peer(r, 0)
+            ).start()
+        back_in[s] = main_motion[0, :, :count_z, :]
+
+    strangers = pl.ds(0, num_struct - 1)
+    all_back = remote(back_in.at[strangers], back_in.at[strangers], back_send, back_recv, peer(1, 0))
+    send_back()
     wide = 2 * LANES
     lane_id = iota((LANES, wide), 0)
     group_id = iota((groups, wide), 0)
 
-    def pair(step, carry):
+    def pair(step):
         j, k = 2 * step // count_z, 2 * step % count_z
         sums = [None] * 3
         for t in range(stencil):
@@ -616,18 +667,19 @@
             line = jnp.sum(sums[c], axis=0, keepdims=True)
             v_wall[c, pl.ds(2 * step, 1), :] = line[:, :LANES]
             v_wall[c, pl.ds(2 * step + 1, 1), :] = line[:, LANES:]
+
+    def pairs(step, carry):
+        for u in range(WALL_STEP):
+            pair(step * WALL_STEP + u)
         return carry
 
     with jax.named_scope("wall"):
-        lax.fori_loop(0, nodes // 2, pair, 0)
+        lax.fori_loop(0, nodes // 2 // WALL_STEP, pairs, 0)
 
     with jax.named_scope("waitwall"):
-        for copy in wall_copies:
-            copy.wait_recv()
+        all_walls.wait_recv()
     with jax.named_scope("edgeinit"):
-        within = lane_deep % COLUMNS
-        inner = ((within >= 1) & (within <= SWEEPS)) | ((within > 2 * SWEEPS) & (within < far_wall))
-        arrived = [jnp.concatenate([wall_in[r, 0], wall_in[r, 1]], axis=0) for r in range(num_struct)]
+        arrived = [jnp.concatenate([wall_in[2 * r], wall_in[2 * r + 1]], axis=0) for r in range(num_struct)]
         for c in range(3):
             total = jnp.zeros((deep, LANES), F32)
             for r in range(num_struct):
@@ -639,22 +691,17 @@
             edge_motion[c] = total
 
     def sweep_edge(step, carry):
-        parts = cell_forces(
-            lambda tet, v, p: edge_grad[9 * tet + 3 * v + p],
-            edge_corners([edge_motion[c] for c in range(3)]),
-            *float_codes(edge_field[3]),
-        )
-        for c, value in enumerate(edge_assemble(parts)):
-            now = edge_motion[c]
-            edge_motion[c] = jnp.where(inner, now - RELAX_FACTOR * value / edge_diag[c], now)
+        open_forces(edge_corners(lambda c: edge_motion[c]), float_codes(edge_field[3]), work.at[0])
+        fill_forces(lambda n, rows: edge_grad[n, rows], work.at[0])
+        for c, value in enumerate(edge_sums()):
+            edge_motion[c] = edge_motion[c] - edge_scale[c] * value
         return carry
 
     with jax.named_scope("sweepedge"):
         lax.fori_loop(0, SWEEPS, sweep_edge, 0)
 
     with jax.named_scope("waitback"):
-        for _, copy in back_copies:
-            copy.wait_recv()
+        all_back.wait_recv()
     with jax.named_scope("outs"):
         for c in range(3):
             for j in range(count_y):
@@ -670,9 +717,8 @@
                 out[c, j, :, wall:] = total + change
 
     with jax.named_scope("waitsend"):
-        for copy in near_copies + wall_copies + [copy for copy, _ in back_copies]:
-            copy.wait_send()
-        all_packs.wait_send()
+        for group in (all_near, all_walls, all_back, all_packs):
+            group.wait_send()
 
 
 def shards(shell_motion, owner, stencil_slot, stencil_weight, prev_motion, node_offset, cell_split):
@@ -704,11 +750,10 @@
         vmem((3 * groups, 2 * LANES), BF16),
         vmem((3, nodes, wall), F32),
         vmem((num_struct, FIELDS, count_z, LANES), F32),
-        vmem((num_struct, 2, FIELDS, count_z, LANES), F32),
-        vmem((num_struct, 2, count_z, LANES), F32),
+        vmem((2 * num_struct, FIELDS, count_z, LANES), F32),
+        vmem((2 * num_struct, count_z, LANES), F32),
         vmem((num_struct, 3, count_z, LANES), F32),
         vmem((num_struct, 4, deep, LANES), F32),
-        vmem((num_struct, 3, deep, LANES), F32),
         vmem((num_struct, 3, deep, LANES), F32),
         vmem((num_struct, 54, deep, LANES), F32),
         vmem((num_struct, 3, deep, LANES), F32),
@@ -716,15 +761,16 @@
         vmem((3, deep, LANES), F32),
         vmem((54, deep, LANES), F32),
         vmem((3, deep, LANES), F32),
+        vmem((num_struct, 2, 24, deep, LANES), F32),
         dma((7,)),
-        dma((num_struct, 3)),
-        dma((num_struct, 3)),
         dma,
         dma,
-        dma((num_struct, 3)),
-        dma((num_struct, 3)),
-        dma((num_struct,)),
-        dma((num_struct,)),
+        dma,
+        dma,
+        dma,
+        dma,
+        dma,
+        dma,
     ]
     return pl.pallas_call(
         functools.partial(window_kernel, (num_struct, num_fluid)),

time: 28.7 us -> 23.8 us (0.83)
  Pallas kernels: 27.9 us -> 23 us
    pallas_call x1, Pallas kernels: 27.9 us -> 23 us  [shards(): pl.pallas_call(functools.partial(window_kernel, (num_struct, num_fluid)),...]
where the time goes in v2:
time: 23.8 us; the launch traced here: 23.6 us
  Pallas kernels  23 us (97%)
  local copies, waits for them, and re-layouts  0.62 us (3%)
    pallas_call x1, Pallas kernels, shards(): pl.pallas_call(functools.partial(window_kernel, (num_struct, num_fluid)),...  23 us
    unnamed x1, local copies, waits for them, and re-layouts  0.62 us

profile of v2, /device:TPU:0, one launch (start us, length us, event | category | flops | bytes accessed | tf_op | source)
XLA Modules:
  0.0 23.6 jit_solution(11108381705573029037)
XLA Ops:
  0.0 23.0 %shard_map.73 = f32[3,2,8,256]{3,2,1,0:T(8,128)S(1)} custom-call(f32[3,8192]{1,0:T(4,128)} %shell.1, s32[64,128]{1,0:T(8,128)} %bitcast.1, s32[4,2,8,128]{3,2,1,0:T(8,128)} %slot.1, f32[4,2,8,128]{3,2,1,0:T(8,128)} %weight.1, f32[3,2,8,256]{3,2,1,0:T(8,128)} %prev.1, f32[3,2,8,256]{3,2,1,0:T(8,128)} %offset.1, s32[2,8,256]{2,1,0:T(8,128)} %split.1), custom_call_target="tpu_custom_call" | custom-call | flops 4294967296 | bytes 16777216 | tf_op jit(solution)/shard_map/pallas_call | solution.py:775
  23.0 0.6 %copy.9 = f32[3,2,8,256]{3,2,1,0:T(8,128)} copy(f32[3,2,8,256]{3,2,1,0:T(8,128)S(1)} %shard_map.73) | data formatting | bytes 98304

commit v3 on v2

--- a/solution.py
+++ b/solution.py
@@ -14,9 +14,9 @@
 STEP_ORDERS = ((0, 1, 2), (0, 2, 1), (1, 0, 2), (1, 2, 0), (2, 0, 1), (2, 1, 0))
 CORNERS = tuple((a, b, c) for a in (0, 1) for b in (0, 1) for c in (0, 1))
 COLUMNS = 16
-FIELDS = 8
-ROW_STEP = 16
+ROW_STEP = 32
 WALL_STEP = 4
+EARLY_PACK = 2
 EARLY_SWEEPS = 2
 MESH = pl.DeviceIdType.MESH
 BF16 = jnp.bfloat16
@@ -209,6 +209,16 @@
     return mask.astype(F32).astype(BF16)
 
 
+def exact_ids(count, width):
+    return iota((count, width), 0).astype(F32).astype(BF16)
+
+
+def equal_hot(ids, row):
+    row = jnp.broadcast_to(row.astype(F32), (16, row.shape[1])).astype(BF16)
+    row = jnp.concatenate([row] * (ids.shape[0] // 16), axis=0)
+    return jnp.where(ids == row, jnp.ones_like(ids), jnp.zeros_like(ids))
+
+
 def place_nodes(devices, capacity, own_ref, place_ref):
     rows = own_ref.shape[0]
     own = own_ref[...]
@@ -243,16 +253,16 @@
     wide = 2 * LANES
     groups = acc_ref.shape[0] // 3
     pair = 16
-    group_id = iota((groups, LANES), 0)
-    lane_id = iota((wide, LANES), 0)
+    group_id = exact_ids(groups, LANES)
+    lane_id = exact_ids(wide, LANES)
 
     def spread(step, carry):
         columns, parts = [], [[] for _ in range(6)]
         for u in range(ROW_STEP):
             row = step * ROW_STEP + u
             at = place_ref[pl.ds(row, 1), :]
-            hit = one_hot(group_id == at // wide)
-            columns.append(one_hot(lane_id == at % wide))
+            hit = equal_hot(group_id, at // wide)
+            columns.append(equal_hot(lane_id, at % wide))
             for c in range(3):
                 value = val_ref[pl.ds(c, 1), pl.ds(pl.multiple_of(row * LANES, LANES), LANES)]
                 value = jnp.broadcast_to(value, (pair, LANES))
@@ -267,6 +277,12 @@
         return carry
 
     lax.fori_loop(first, last, spread, 0)
+
+
+def strips(num_struct, count_y, free):
+    strip = free // num_struct + 2 * SWEEPS
+    per_tile = LANES // strip
+    return strip, per_tile, -(-num_struct * count_y // per_tile), -(-7 * count_y // per_tile)
 
 
 def window_kernel(
@@ -294,7 +310,9 @@
     v_wall,
     tiles,
     near_in,
+    edge_in,
     wall_in,
+    back_out,
     back_in,
     main_field,
     main_motion,
@@ -308,6 +326,8 @@
     local_sem,
     near_send,
     near_recv,
+    edge_send,
+    edge_recv,
     pack_send,
     pack_recv,
     wall_send,
@@ -324,8 +344,9 @@
     nodes = count_y * count_z
     deep = 2 * count_z
     span = count_y * COLUMNS
-    pitch = LANES // count_y
     share = free // num_struct
+    rows_all = num_struct * count_y
+    strip, per_tile, main_tiles, near_tiles = strips(num_struct, count_y, free)
     rows_own = v_owner.shape[0]
     capacity = 2 * rows_own * LANES // devices
     pieces = capacity // LANES
@@ -355,14 +376,10 @@
 
     barrier = pltpu.get_barrier_semaphore()
 
-    def greet(d, carry):
-        other = (me + d) % devices
-        pl.semaphore_signal(
-            barrier, inc=1, device_id=(other // num_fluid, other % num_fluid), device_id_type=MESH
-        )
-        return carry
-
-    lax.fori_loop(1, devices, greet, 0)
+    shifts = sorted(range(num_fluid), key=lambda d: -min(d, num_fluid - d))
+    everyone = [peer(ds, df) for ds in range(num_struct) for df in shifts if (ds, df) != (0, 0)]
+    for to in everyone:
+        pl.semaphore_signal(barrier, inc=1, device_id=to, device_id_type=MESH)
 
     with jax.named_scope("place"):
         loads[0].wait()
@@ -373,8 +390,8 @@
         for load in loads[1:4]:
             load.wait()
         slab = jnp.zeros((count_z, LANES), F32)
+        joined = [[None] * near_tiles for _ in range(num_struct)]
         for n in range(7):
-            shifted = [[None] * count_y for _ in range(num_struct)]
             for j in range(count_y):
                 if n < 3:
                     near, far = v_offset[n, j, :, :wall], v_offset[n, j, :, wall:]
@@ -387,9 +404,11 @@
                     line = far
                     if begin < 0:
                         line = jnp.where(lane >= LANES + begin, near, far)
-                    if begin + pitch > LANES:
-                        line = jnp.where(lane < begin + pitch - LANES, near, far)
-                    shifted[q][j] = turn(line, pitch * j - begin, 1)
+                    if begin + strip > LANES:
+                        line = jnp.where(lane < begin + strip - LANES, near, far)
+                    t, m = divmod(n * count_y + j, per_tile)
+                    line = turn(line, strip * m - begin, 1)
+                    joined[q][t] = jnp.where(lane >= strip * m, line, joined[q][t]) if m else line
                 if n < 4:
                     base = span * n + COLUMNS * j
                     low = turn(jnp.where(lane == LANES - 1, near, far), base + 1, 1)
@@ -398,14 +417,16 @@
                     slab = jnp.where(
                         (lane >= base + 2 * SWEEPS) & (lane < base + COLUMNS), high, slab
                     )
-            for q in range(num_struct):
-                total = shifted[q][0]
-                for j in range(1, count_y):
-                    total = jnp.where(lane >= pitch * j, shifted[q][j], total)
-                tiles[q, n] = total
         for q in range(num_struct):
-            tiles[q, 7] = slab
-
+            for t in range(near_tiles):
+                tiles[q, t] = joined[q][t]
+        edge_in[0] = slab
+
+    steps = rows_own // ROW_STEP
+    with jax.named_scope("packfirst"):
+        acc[...] = jnp.zeros_like(acc)
+        loads[4].wait()
+        pack_nodes(0, EARLY_PACK, place, v_shell, acc)
     with jax.named_scope("barrier"):
         pl.semaphore_wait(barrier, devices - 1)
 
@@ -424,16 +445,30 @@
             to,
         )
 
+    others = pl.ds(1, 2 * num_struct - 1)
+    def spread_copy(buffer, send, recv, r, df):
+        return remote(
+            buffer.at[0, planes_of(df)],
+            buffer.at[2 * r + (df != 0), planes_of(df)],
+            send,
+            recv,
+            peer(-r, -df),
+        )
+
+    def send_around(buffer, send, recv):
+        for r, df in around:
+            spread_copy(buffer, send, recv, r, df).start()
+        return remote(buffer.at[others], buffer.at[others], send, recv, peer(1, 0))
+
+    all_edges = send_around(edge_in, edge_send, edge_recv)
     for r, df in around:
         near_copy(r, df).start()
-    others = pl.ds(1, 2 * num_struct - 1)
     all_near = remote(near_in.at[others], near_in.at[others], near_send, near_recv, peer(1, 0))
     near_in[0] = tiles[s]
 
+
     with jax.named_scope("pack"):
-        acc[...] = jnp.zeros_like(acc)
-        loads[4].wait()
-        pack_nodes(0, rows_own // ROW_STEP, place, v_shell, acc)
+        pack_nodes(EARLY_PACK, steps, place, v_shell, acc)
     with jax.named_scope("relay"):
         pack_groups = groups // 2
         for o in range(devices):
@@ -446,18 +481,8 @@
 
     with jax.named_scope("sendpack"):
 
-        def send_pack(d, carry):
-            other = (me + d) % devices
-            remote(
-                packed.at[other],
-                received.at[me],
-                pack_send,
-                pack_recv,
-                (other // num_fluid, other % num_fluid),
-            ).start()
-            return carry
-
-        lax.fori_loop(1, devices, send_pack, 0)
+        for to in everyone:
+            remote(packed.at[to[0] * num_fluid + to[1]], received.at[me], pack_send, pack_recv, to).start()
         received[me] = packed[me]
     all_packs = remote(
         packed.at[pl.ds(0, devices - 1)],
@@ -468,53 +493,58 @@
     )
 
     lane_deep = iota((deep, LANES), 1)
-    row_low = lane_deep < pitch
-    column = lane_deep % pitch + share * s
+    column = lane_deep % strip + share * s
     within = lane_deep % COLUMNS
     inner = ((within >= 1) & (within <= SWEEPS)) | ((within > 2 * SWEEPS) & (within < far_wall))
-    free_node = (column >= SWEEPS) & (column < free + SWEEPS)
+    free_node = (column >= SWEEPS) & (column < free + SWEEPS) & (lane_deep < strip * per_tile)
+
+    tail = [strip * (min(per_tile, rows_all - per_tile * t) - 1) for t in range(main_tiles)]
 
     def main_corners(read):
-        values = [[read(r, c) for c in range(3)] for r in range(num_struct)]
-        moved = [[[turn(p, n, 1) for p in row] for row in values] for n in (-1, pitch, pitch - 1)]
-        for r in range(num_struct):
+        values = [[read(t, c) for c in range(3)] for t in range(main_tiles)]
+        for t, here in enumerate(values):
+            following = values[(t + 1) % main_tiles]
             high = [
-                [jnp.where(row_low, p, q) for p, q in zip(moved[n][r], moved[n][(r + 1) % num_struct])]
-                for n in (1, 2)
+                [
+                    jnp.where(lane_deep < tail[t], turn(p, -strip - a, 1), turn(q, tail[t] - a, 1))
+                    for p, q in zip(here, following)
+                ]
+                for a in (0, 1)
             ]
-            yield r, with_planes(
-                {(0, 0): values[r], (1, 0): moved[0][r], (0, 1): high[0], (1, 1): high[1]}
-            )
+            near = [turn(p, -1, 1) for p in here]
+            yield t, with_planes({(0, 0): here, (1, 0): near, (0, 1): high[0], (1, 1): high[1]})
 
     def main_sums():
-        lows, highs = [], []
-        for r in range(num_struct):
-            ends = close_cells(work.at[r], float_codes(main_field[r, 3]))
+        lows, insides, outsides = [], [], []
+        for t in range(main_tiles):
+            ends = close_cells(work.at[t], float_codes(main_field[t, 3]))
             lows.append([p + turn(q, 1, 1) for p, q in zip(ends[0, 0], ends[1, 0])])
-            highs.append(
-                [turn(p, pitch, 1) + turn(q, pitch + 1, 1) for p, q in zip(ends[0, 1], ends[1, 1])]
-            )
-        for r in range(num_struct):
-            yield r, [
-                p + jnp.where(row_low, before, now) for p, before, now in zip(lows[r], highs[r - 1], highs[r])
+            upper = list(zip(ends[0, 1], ends[1, 1]))
+            insides.append([turn(p, strip, 1) + turn(q, strip + 1, 1) for p, q in upper])
+            outsides.append([turn(p, -tail[t], 1) + turn(q, 1 - tail[t], 1) for p, q in upper])
+        for t in range(main_tiles):
+            yield t, [
+                p + jnp.where(lane_deep < strip, before, now)
+                for p, before, now in zip(lows[t], outsides[t - 1], insides[t])
             ]
 
     def prepare_main():
-        for r in range(num_struct):
-            for n in range(FIELDS):
-                whole = jnp.concatenate([near_in[2 * r, n], near_in[2 * r + 1, n]], axis=0)
+        source = [
+            [jnp.concatenate([near_in[2 * r, t], near_in[2 * r + 1, t]], axis=0) for t in range(near_tiles)]
+            for r in range(num_struct)
+        ]
+        for n in range(7):
+            for t in range(main_tiles):
+                total = None
+                for m in range(min(per_tile, rows_all - per_tile * t)):
+                    r, j = divmod(per_tile * t + m, count_y)
+                    k, at = divmod(n * count_y + j, per_tile)
+                    moved = turn(source[r][k], strip * (m - at), 1)
+                    total = jnp.where(lane_deep >= strip * m, moved, total) if m else moved
                 if n < 4:
-                    main_field[r, n] = whole
-                elif n < 7:
-                    main_motion[r, n - 4] = whole
+                    main_field[t, n] = total
                 else:
-                    for m in range(4):
-                        moved = turn(whole, span * (r - m), 1)
-                        if r == 0:
-                            edge_field[m] = moved
-                        else:
-                            edge_field[m] = jnp.where(lane_deep >= span * r, moved, edge_field[m])
-
+                    main_motion[t, n - 4] = total
         for r, corners in main_corners(lambda at, c: main_field[at, c]):
             open_gradients(corners, float_codes(main_field[r, 3]), work.at[r])
 
@@ -525,7 +555,7 @@
             fill_gradients(work.at[r], put)
             return carry
 
-        lax.fori_loop(0, num_struct, row, 0)
+        lax.fori_loop(0, main_tiles, row, 0)
         for r, values in main_sums():
             for c in range(3):
                 main_scale[r, c] = jnp.where(free_node, RELAX_FACTOR / values[c], 0.0)
@@ -534,7 +564,7 @@
         for r, corners in main_corners(lambda at, c: main_motion[at, c]):
             open_forces(corners, float_codes(main_field[r, 3]), work.at[r])
 
-        for r in range(num_struct):
+        for r in range(main_tiles):
             fill_forces(lambda n, rows: main_grad[r, n, rows], work.at[r])
         for r, values in main_sums():
             for c in range(3):
@@ -553,6 +583,13 @@
         return [(p + q) + (u + v) for p, q, u, v in zip(*moved)]
 
     def prepare_edge():
+        for r in range(num_struct):
+            whole = jnp.concatenate([edge_in[2 * r], edge_in[2 * r + 1]], axis=0)
+            for n in range(4):
+                moved = turn(whole, span * (r - n), 1)
+                if r > 0:
+                    moved = jnp.where(lane_deep >= span * r, moved, edge_field[n])
+                edge_field[n] = moved
         open_gradients(edge_corners(lambda c: edge_field[c]), float_codes(edge_field[3]), work.at[0])
 
         def put(n, rows, value):
@@ -575,19 +612,20 @@
                 total = part if total is None else total + part
         return jnp.sum(total, axis=0, keepdims=True)
 
+    with jax.named_scope("prepedge"):
+        all_edges.wait_recv()
+        prepare_edge()
+    with jax.named_scope("points"):
+        loads[5].wait()
+        loads[6].wait()
+        plane_slot, plane_weight = plane_points(v_slot, 0), plane_points(v_weight, 0.0)
+
     with jax.named_scope("waitnear"):
         all_near.wait_recv()
     with jax.named_scope("prepmain"):
         prepare_main()
     with jax.named_scope("sweeps"):
         lax.fori_loop(0, EARLY_SWEEPS, sweep_main, 0)
-    with jax.named_scope("prepedge"):
-        prepare_edge()
-    with jax.named_scope("points"):
-        loads[5].wait()
-        loads[6].wait()
-        plane_slot, plane_weight = plane_points(v_slot, 0), plane_points(v_weight, 0.0)
-
     with jax.named_scope("waitpack"):
         all_packs.wait_recv()
 
@@ -615,34 +653,29 @@
             tile = jnp.where((lane >= span * c) & (lane < span * (c + 1)), spread, tile)
         wall_in[0] = tile
 
-    def wall_copy(r, df):
-        return remote(
-            wall_in.at[0, planes_of(df)],
-            wall_in.at[2 * r + (df != 0), planes_of(df)],
-            wall_send,
-            wall_recv,
-            peer(-r, -df),
-        )
-
-    for r, df in around:
-        wall_copy(r, df).start()
-    all_walls = remote(wall_in.at[others], wall_in.at[others], wall_send, wall_recv, peer(1, 0))
+    all_walls = send_around(wall_in, wall_send, wall_recv)
 
     with jax.named_scope("latesweeps"):
         lax.fori_loop(EARLY_SWEEPS, SWEEPS, sweep_main, 0)
 
     def send_back():
+        for r in range(num_struct):
+            for c in range(3):
+                total = None
+                for j in range(count_y):
+                    t, m = divmod(r * count_y + j, per_tile)
+                    moved = turn(main_motion[t, c, :count_z, :], strip * (j - m), 1)
+                    total = jnp.where(lane >= strip * j, moved, total) if j else moved
+                back_out[r, c] = total
         for r in range(1, num_struct):
-            remote(
-                main_motion.at[r, :, pl.ds(0, count_z)], back_in.at[s], back_send, back_recv, peer(r, 0)
-            ).start()
-        back_in[s] = main_motion[0, :, :count_z, :]
+            remote(back_out.at[r], back_in.at[s], back_send, back_recv, peer(r, 0)).start()
+        back_in[s] = back_out[0]
 
     strangers = pl.ds(0, num_struct - 1)
     all_back = remote(back_in.at[strangers], back_in.at[strangers], back_send, back_recv, peer(1, 0))
     send_back()
     wide = 2 * LANES
-    lane_id = iota((LANES, wide), 0)
+    lane_id = exact_ids(LANES, wide)
     group_id = iota((groups, wide), 0)
 
     def pair(step):
@@ -655,7 +688,7 @@
             by = jnp.concatenate(
                 [v_weight[t, j, pl.ds(k, 1), :], v_weight[t, j, pl.ds(k + 1, 1), :]], axis=1
             )
-            choose = one_hot(lane_id == at % LANES)
+            choose = equal_hot(lane_id, at % LANES)
             values = jnp.dot(
                 both[...], jnp.concatenate([choose, choose], axis=0), preferred_element_type=F32
             )
@@ -708,7 +741,7 @@
                 out[c, j, :, :wall] = v_wall[c, pl.ds(j * count_z, count_z), :]
                 total = None
                 for q in range(num_struct):
-                    moved = turn(back_in[q, c], share * q - pitch * j - SWEEPS, 1)
+                    moved = turn(back_in[q, c], share * q - strip * j - SWEEPS, 1)
                     total = moved if total is None else jnp.where(lane >= share * q, moved, total)
                 delta = edge_motion[c, :count_z, :]
                 low = turn(delta, -1 - COLUMNS * j, 1)
@@ -717,7 +750,7 @@
                 out[c, j, :, wall:] = total + change
 
     with jax.named_scope("waitsend"):
-        for group in (all_near, all_walls, all_back, all_packs):
+        for group in (all_near, all_edges, all_walls, all_back, all_packs):
             group.wait_send()
 
 
@@ -733,7 +766,8 @@
     nodes, deep = count_y * count_z, 2 * count_z
     assert wall == free == LANES and count_z == 2 * SWEEPS == 8 and num_struct >= 2 and num_fluid >= 3
     assert num_struct * count_y * COLUMNS == LANES and 2 * stencil * nodes == LANES
-    assert free // num_struct + 2 * SWEEPS <= LANES // count_y
+    strip, per_tile, main_tiles, near_tiles = strips(num_struct, count_y, free)
+    assert count_y <= per_tile and num_struct * count_y > per_tile
     vmem, dma = pltpu.VMEM, pltpu.SemaphoreType.DMA
     scratch = [
         vmem((3, own), F32),
@@ -749,20 +783,24 @@
         vmem((devices, 3 * pieces, LANES), F32),
         vmem((3 * groups, 2 * LANES), BF16),
         vmem((3, nodes, wall), F32),
-        vmem((num_struct, FIELDS, count_z, LANES), F32),
-        vmem((2 * num_struct, FIELDS, count_z, LANES), F32),
+        vmem((num_struct, near_tiles, count_z, LANES), F32),
+        vmem((2 * num_struct, near_tiles, count_z, LANES), F32),
+        vmem((2 * num_struct, count_z, LANES), F32),
         vmem((2 * num_struct, count_z, LANES), F32),
         vmem((num_struct, 3, count_z, LANES), F32),
-        vmem((num_struct, 4, deep, LANES), F32),
-        vmem((num_struct, 3, deep, LANES), F32),
-        vmem((num_struct, 54, deep, LANES), F32),
-        vmem((num_struct, 3, deep, LANES), F32),
+        vmem((num_struct, 3, count_z, LANES), F32),
+        vmem((main_tiles, 4, deep, LANES), F32),
+        vmem((main_tiles, 3, deep, LANES), F32),
+        vmem((main_tiles, 54, deep, LANES), F32),
+        vmem((main_tiles, 3, deep, LANES), F32),
         vmem((4, deep, LANES), F32),
         vmem((3, deep, LANES), F32),
         vmem((54, deep, LANES), F32),
         vmem((3, deep, LANES), F32),
-        vmem((num_struct, 2, 24, deep, LANES), F32),
+        vmem((main_tiles, 2, 24, deep, LANES), F32),
         dma((7,)),
+        dma,
+        dma,
         dma,
         dma,
         dma,

time: 23.8 us -> 22.2 us (0.933)
  Pallas kernels: 23 us -> 21.4 us
    pallas_call x1, Pallas kernels: 23 us -> 21.4 us  [shards(): pl.pallas_call(functools.partial(window_kernel, (num_struct, num_fluid)),...]
where the time goes in v3:
time: 22.2 us; the launch traced here: 22 us
  Pallas kernels  21.4 us (96%)
  local copies, waits for them, and re-layouts  0.62 us (3%)
    pallas_call x1, Pallas kernels, shards(): pl.pallas_call(functools.partial(window_kernel, (num_struct, num_fluid)),...  21.4 us
    unnamed x1, local copies, waits for them, and re-layouts  0.62 us

profile of v3, /device:TPU:0, one launch (start us, length us, event | category | flops | bytes accessed | tf_op | source)
XLA Modules:
  0.0 22.0 jit_solution(1291347063756362563)
XLA Ops:
  0.0 21.4 %shard_map.73 = f32[3,2,8,256]{3,2,1,0:T(8,128)S(1)} custom-call(f32[3,8192]{1,0:T(4,128)} %shell.1, s32[64,128]{1,0:T(8,128)} %bitcast.1, s32[4,2,8,128]{3,2,1,0:T(8,128)} %slot.1, f32[4,2,8,128]{3,2,1,0:T(8,128)} %weight.1, f32[3,2,8,256]{3,2,1,0:T(8,128)} %prev.1, f32[3,2,8,256]{3,2,1,0:T(8,128)} %offset.1, s32[2,8,256]{2,1,0:T(8,128)} %split.1), custom_call_target="tpu_custom_call" | custom-call | flops 4294967296 | bytes 16777216 | tf_op jit(solution)/shard_map/pallas_call | solution.py:813
  21.4 0.6 %copy.9 = f32[3,2,8,256]{3,2,1,0:T(8,128)} copy(f32[3,2,8,256]{3,2,1,0:T(8,128)S(1)} %shard_map.73) | data formatting | bytes 98304

commit v4 on v3

--- a/solution.py
+++ b/solution.py
@@ -15,8 +15,7 @@
 CORNERS = tuple((a, b, c) for a in (0, 1) for b in (0, 1) for c in (0, 1))
 COLUMNS = 16
 ROW_STEP = 32
-WALL_STEP = 4
-EARLY_PACK = 2
+WALL_STEP = 8
 EARLY_SWEEPS = 2
 MESH = pl.DeviceIdType.MESH
 BF16 = jnp.bfloat16
@@ -222,6 +221,7 @@
 def place_nodes(devices, capacity, own_ref, place_ref):
     rows = own_ref.shape[0]
     own = own_ref[...]
+    ids = own.astype(F32).astype(BF16)
     upper = iota((LANES, LANES), 0) < iota((LANES, LANES), 1)
     prefix = jnp.concatenate([one_hot(upper), jnp.ones((LANES, LANES), BF16)], axis=0)
     lower = one_hot(iota((rows, rows), 1) < iota((rows, rows), 0))
@@ -229,7 +229,10 @@
 
     def ranks(step, place):
         masks = [own == step * chunk + o for o in range(chunk)]
-        named = [one_hot(mask) for mask in masks]
+        named = [
+            jnp.where(ids == (step * chunk + o) * 1.0, jnp.ones_like(ids), jnp.zeros_like(ids))
+            for o in range(chunk)
+        ]
         above = jnp.dot(lower, jnp.concatenate(named, axis=1), preferred_element_type=F32).astype(BF16)
         left = [
             jnp.concatenate([named[o], above[:, o * LANES : (o + 1) * LANES]], axis=1) for o in range(chunk)
@@ -381,6 +384,7 @@
     for to in everyone:
         pl.semaphore_signal(barrier, inc=1, device_id=to, device_id_type=MESH)
 
+    acc[...] = jnp.zeros_like(acc)
     with jax.named_scope("place"):
         loads[0].wait()
         place_nodes(devices, capacity, v_owner, place)
@@ -422,15 +426,22 @@
                 tiles[q, t] = joined[q][t]
         edge_in[0] = slab
 
-    steps = rows_own // ROW_STEP
-    with jax.named_scope("packfirst"):
-        acc[...] = jnp.zeros_like(acc)
+    with jax.named_scope("pack"):
         loads[4].wait()
-        pack_nodes(0, EARLY_PACK, place, v_shell, acc)
+        pack_nodes(0, rows_own // ROW_STEP, place, v_shell, acc)
+    with jax.named_scope("relay"):
+        pack_groups = groups // 2
+        for o in range(devices):
+            for c in range(3):
+                for b in range(pieces):
+                    m = o * pieces + b
+                    packed[o, pl.ds(c * pieces + b, 1), :] = acc[
+                        pl.ds(c * pack_groups + m // 2, 1), pl.ds((m % 2) * LANES, LANES)
+                    ]
     with jax.named_scope("barrier"):
         pl.semaphore_wait(barrier, devices - 1)
 
-    around = [(r, df) for r in range(num_struct) for df in (0, -1, 1) if (r, df) != (0, 0)]
+    around = [(r, df) for df in (-1, 1, 0) for r in range(num_struct) if (r, df) != (0, 0)]
 
     def planes_of(df):
         return pl.ds(0, count_z) if df == 0 else pl.ds(0 if df > 0 else SWEEPS, SWEEPS)
@@ -466,18 +477,6 @@
     all_near = remote(near_in.at[others], near_in.at[others], near_send, near_recv, peer(1, 0))
     near_in[0] = tiles[s]
 
-
-    with jax.named_scope("pack"):
-        pack_nodes(EARLY_PACK, steps, place, v_shell, acc)
-    with jax.named_scope("relay"):
-        pack_groups = groups // 2
-        for o in range(devices):
-            for c in range(3):
-                for b in range(pieces):
-                    m = o * pieces + b
-                    packed[o, pl.ds(c * pieces + b, 1), :] = acc[
-                        pl.ds(c * pack_groups + m // 2, 1), pl.ds((m % 2) * LANES, LANES)
-                    ]
 
     with jax.named_scope("sendpack"):
 

time: 22.2 us -> 21.9 us (0.986)
  Pallas kernels: 21.4 us -> 21.1 us
    pallas_call x1, Pallas kernels: 21.4 us -> 21.1 us  [shards(): pl.pallas_call(functools.partial(window_kernel, (num_struct, num_fluid)),...]
where the time goes in v4:
time: 21.9 us; the launch traced here: 21.8 us
  Pallas kernels  21.1 us (96%)
  local copies, waits for them, and re-layouts  0.62 us (3%)
    pallas_call x1, Pallas kernels, shards(): pl.pallas_call(functools.partial(window_kernel, (num_struct, num_fluid)),...  21.1 us
    unnamed x1, local copies, waits for them, and re-layouts  0.62 us

profile of v4, /device:TPU:0, one launch (start us, length us, event | category | flops | bytes accessed | tf_op | source)
XLA Modules:
  0.0 21.8 jit_solution(8762790246503205650)
XLA Ops:
  0.0 21.1 %shard_map.73 = f32[3,2,8,256]{3,2,1,0:T(8,128)S(1)} custom-call(f32[3,8192]{1,0:T(4,128)} %shell.1, s32[64,128]{1,0:T(8,128)} %bitcast.1, s32[4,2,8,128]{3,2,1,0:T(8,128)} %slot.1, f32[4,2,8,128]{3,2,1,0:T(8,128)} %weight.1, f32[3,2,8,256]{3,2,1,0:T(8,128)} %prev.1, f32[3,2,8,256]{3,2,1,0:T(8,128)} %offset.1, s32[2,8,256]{2,1,0:T(8,128)} %split.1), custom_call_target="tpu_custom_call" | custom-call | flops 4294967296 | bytes 16777216 | tf_op jit(solution)/shard_map/pallas_call | solution.py:812
  21.2 0.6 %copy.9 = f32[3,2,8,256]{3,2,1,0:T(8,128)} copy(f32[3,2,8,256]{3,2,1,0:T(8,128)S(1)} %shard_map.73) | data formatting | bytes 98304
